TPU v7x, 128 devices: a whole 4x4x4 slice. The times are simulated.
128 devices in a mesh: model: 4 (over x), data: 32 (over z, y, core).
Axes of the slice: x: 4, y: 4, z: 4, core: 2. Of those that a mesh axis runs over, the one named last changes fastest.
Arguments:
- grad_in: bfloat16 [32, 4, 768, 3072], P('data', None, None, 'model')
- w_in: float32 [4, 768, 3072], P(None, 'data', 'model')
- row_in: float32 [4, 768], P(None, 'data')
- col_in: float32 [4, 3072], P(None, 'model')
- grad_out: bfloat16 [32, 2, 3072, 768], P('data', None, 'model')
- w_out: float32 [2, 3072, 768], P(None, 'model', 'data')
- row_out: float32 [2, 3072], P(None, 'model')
- col_out: float32 [2, 768], P(None, 'data')
- grad_qkv: bfloat16 [32, 9, 768, 768], P('data', None, None, 'model')
- w_qkv: float32 [9, 768, 768], P(None, 'data', 'model')
- row_qkv: float32 [9, 768], P(None, 'data')
- col_qkv: float32 [9, 768], P(None, 'model')
- grad_o: bfloat16 [32, 3, 768, 768], P('data', None, 'model')
- w_o: float32 [3, 768, 768], P(None, 'model', 'data')
- row_o: float32 [3, 768], P(None, 'model')
- col_o: float32 [3, 768], P(None, 'data')
Outputs:
- output 1: float32 [4, 768, 3072], P(None, 'data', 'model')
- output 2: float32 [4, 768], P(None, 'data')
- output 3: float32 [4, 3072], P(None, 'model')
- output 4: float32 [2, 3072, 768], P(None, 'model', 'data')
- output 5: float32 [2, 3072], P(None, 'model')
- output 6: float32 [2, 768], P(None, 'data')
- output 7: float32 [9, 768, 768], P(None, 'data', 'model')
- output 8: float32 [9, 768], P(None, 'data')
- output 9: float32 [9, 768], P(None, 'model')
- output 10: float32 [3, 768, 768], P(None, 'model', 'data')
- output 11: float32 [3, 768], P(None, 'model')
- output 12: float32 [3, 768], P(None, 'data')
All inputs are finite; a program needn't handle non-finite values.
Results may differ from a plain program's by a relative error of at most 0.001.
Values sent between devices are 32-bit elements.
A program may use at most 1 GiB of HBM per device.

v0:
```python
import jax
import jax.numpy as jnp
from jax import lax
from jax.sharding import PartitionSpec as P, NamedSharding

OPT_STEP = 4
EPS_SQ = 1e-30
BETA_TWO = 1.0 - OPT_STEP ** -0.8
LR_BASE = min(1e-2, OPT_STEP ** -0.5)


def finish_update(grad_mean, weight, row_mom, col_mom, row_sum, col_sum, row_axis, full_rows, full_cols):
    new_row = BETA_TWO * row_mom + (1.0 - BETA_TWO) * (row_sum / full_cols)
    new_col = BETA_TWO * col_mom + (1.0 - BETA_TWO) * (col_sum / full_rows)
    row_mean = lax.psum(jnp.sum(new_row, axis=1, keepdims=True), row_axis) / full_rows
    update = grad_mean / jnp.sqrt((new_row / row_mean)[:, :, None] * new_col[:, None, :])
    upd_sq = lax.psum(jnp.sum(update * update, axis=(1, 2), keepdims=True), ('model', 'data'))
    update = update / jnp.maximum(1.0, jnp.sqrt(upd_sq / (full_rows * full_cols)))
    w_sq = lax.psum(jnp.sum(weight * weight, axis=(1, 2), keepdims=True), ('model', 'data'))
    w_rms = jnp.sqrt(w_sq / (full_rows * full_cols))
    return weight - LR_BASE * jnp.maximum(1e-3, w_rms) * update, new_row, new_col


def update_block(grad_parts, weight, row_mom, col_mom, rows_on_data, axis_sizes):
    if rows_on_data:
        row_axis, col_axis, scatter_dim = 'data', 'model', 1
    else:
        row_axis, col_axis, scatter_dim = 'model', 'data', 2
    full_rows = weight.shape[1] * axis_sizes[row_axis]
    full_cols = weight.shape[2] * axis_sizes[col_axis]
    part_sum = lax.psum_scatter(grad_parts[0].astype(jnp.float32), 'data', scatter_dimension=scatter_dim, tiled=True)
    grad_mean = part_sum / axis_sizes['data']
    grad_sq = grad_mean * grad_mean + EPS_SQ
    row_sum = lax.psum(jnp.sum(grad_sq, axis=2), col_axis)
    col_sum = lax.psum(jnp.sum(grad_sq, axis=1), row_axis)
    return finish_update(grad_mean, weight, row_mom, col_mom, row_sum, col_sum, row_axis, full_rows, full_cols)


def solution(mesh):
    axis_sizes = dict(mesh.shape)
    rows_data = (P('data', None, None, 'model'), P(None, 'data', 'model'), P(None, 'data'), P(None, 'model'))
    rows_model = (P('data', None, 'model', None), P(None, 'model', 'data'), P(None, 'model'), P(None, 'data'))

    def step_all(grad_in, w_in, row_in, col_in, grad_out, w_out, row_out, col_out,
                 grad_qkv, w_qkv, row_qkv, col_qkv, grad_o, w_o, row_o, col_o):
        w_in_new, row_in_new, col_in_new = update_block(grad_in, w_in, row_in, col_in, True, axis_sizes)
        w_out_new, row_out_new, col_out_new = update_block(grad_out, w_out, row_out, col_out, False, axis_sizes)
        w_qkv_new, row_qkv_new, col_qkv_new = update_block(grad_qkv, w_qkv, row_qkv, col_qkv, True, axis_sizes)
        w_o_new, row_o_new, col_o_new = update_block(grad_o, w_o, row_o, col_o, False, axis_sizes)
        return (w_in_new, row_in_new, col_in_new, w_out_new, row_out_new, col_out_new,
                w_qkv_new, row_qkv_new, col_qkv_new, w_o_new, row_o_new, col_o_new)

    in_specs = rows_data + rows_model + rows_data + rows_model
    out_specs = rows_data[1:] + rows_model[1:] + rows_data[1:] + rows_model[1:]
    return jax.shard_map(step_all, mesh=mesh, in_specs=in_specs, out_specs=out_specs, check_vma=False)
```

profile of v0, /device:TPU:0, one launch (start us, length us, event | category | flops | bytes accessed | tf_op | source)
XLA Modules:
  0.0 601.3 jit_solution(14649296279218409698)
XLA Ops:
  7.2 1.5 copy.30
  8.8 1.7 bitcast_convert_fusion.3
  10.5 2.8 copy.28
  13.3 2.5 bitcast_convert_fusion.2
  15.9 4.3 copy.29
  20.1 3.5 bitcast_convert_fusion.1
  23.7 6.8 %bitcast_convert_fusion = f32[4,768,768]{2,1,0:T(8,128)} fusion(bf16[1,4,768,768]{3,2,1,0:T(8,128)(2,1)} %param.16), kind=kLoop, calls=%fused_computation | loop fusion | flops 2359296 | bytes 14155776 | tf_op jit(solution)/shard_map/convert_element_type | solution.py:31
  31.9 61.8 %reduce-scatter.11.cloned.1.call-done = f32[3,192,24]{1,2,0:T(8,128)} async-done(((f32[3,192,768]{1,2,0:T(8,128)}), f32[3,192,24]{1,2,0:T(8,128)}) %reduce-scatter.11.cloned.1.call-update) | async-done | bytes 55312 | tf_op jit(solution)/shard_map/reduce_scatter | solution.py:31
  94.7 86.2 %reduce-scatter.7.cloned.1.call-done = f32[2,768,24]{1,2,0:T(8,128)} async-done(((f32[2,768,768]{1,2,0:T(8,128)}), f32[2,768,24]{1,2,0:T(8,128)}) %reduce-scatter.7.cloned.1.call-update) | async-done | bytes 147472 | tf_op jit(solution)/shard_map/reduce_scatter | solution.py:31
  181.9 90.2 %reduce-scatter.9.cloned.1.call-done = f32[9,24,192]{2,1,0:T(8,128)} async-done(((f32[9,768,192]{2,1,0:T(8,128)}), f32[9,24,192]{2,1,0:T(8,128)}) %reduce-scatter.9.cloned.1.call-update) | async-done | bytes 165904 | tf_op jit(solution)/shard_map/reduce_scatter | solution.py:31
  273.1 97.5 %reduce-scatter.5.cloned.1.call-done = f32[4,24,768]{2,1,0:T(8,128)} async-done(((f32[4,768,768]{2,1,0:T(8,128)}), f32[4,24,768]{2,1,0:T(8,128)}) %reduce-scatter.5.cloned.1.call-update) | async-done | bytes 294928 | tf_op jit(solution)/shard_map/reduce_scatter | solution.py:31
  370.7 1.1 fusion.1
  371.8 16.8 %all-reduce.3 = (f32[4,24]{1,0:T(4,128)S(1)}, f32[9,24]{1,0:T(8,128)S(1)}) all-reduce(f32[4,24]{1,0:T(4,128)S(1)} %get-tuple-element.12, f32[9,24]{1,0:T(8,128)S(1)} %get-tuple-element.14), channel_id=1, replica_groups=mesh['model'=4,'data'=32] {'model'}, use_global_device_ids=true, to_apply=%region_4.0 | all-reduce | flops 312 | bytes 2496 | tf_op jit(solution)/shard_map/psum | solution.py:34
  388.8 123.8 %all-reduce.1 = (f32[4,768]{1,0:T(4,128)S(1)}, f32[4,1]{0,1:T(1,128)S(1)}, f32[2,768]{1,0:T(2,128)S(1)}, f32[9,192]{1,0:T(8,128)S(1)}, f32[9,1]{0,1:T(1,128)S(1)}, /*index=5*/f32[3,192]{1,0:T(4,128)S(1)}) all-reduce(f32[4,768]{1,0:T(4,128)S(1)} %get-tuple-element.13, ...), channel_id=1, replica_groups=mesh['model'=4,'data'=32] {'data'}, use_global_device_ids=true, to_apply=%region_8.0 | all-reduce | flops 6925 | bytes 55400 | tf_op jit(solution)/shard_map/psum | solution.py:35
  512.9 7.7 %all-reduce.2 = (f32[2,24]{1,0:T(2,128)S(1)}, f32[2,1]{0,1:T(1,128)S(1)}, f32[3,24]{1,0:T(4,128)S(1)}, f32[3,1]{0,1:T(1,128)S(1)}) all-reduce(f32[2,24]{1,0:T(2,128)S(1)} %get-tuple-element.17, f32[2,1]{0,1:T(1,128)S(1)} %bitcast.58, f32[3,24]{1,0:T(4,128)S(1)} %get-tuple-element.19, ...), channel_id=1, replica_groups=mesh['model'=4,'data'=32] {'model'}, use_global_device_ids=true, to_apply=%region_19.0 | all-reduce | flops 125 | bytes 1000 | tf_op jit(solution)/shard_map/psum | solution.py:35
  521.1 1.1 multiply_reduce_fusion.6
  522.2 1.1 multiply_reduce_fusion.4
  523.3 1.2 multiply_reduce_fusion.2
  524.4 1.2 multiply_reduce_fusion
  525.6 62.1 %all-reduce = (f32[4,1,1]{0,2,1:T(1,128)S(1)}, f32[4,1,1]{0,2,1:T(1,128)S(1)}, f32[2,1,1]{0,2,1:T(1,128)S(1)}, f32[2,1,1]{0,2,1:T(1,128)S(1)}, f32[9,1,1]{0,2,1:...) all-reduce(f32[4,1,1]{0,2,1:T(1,128)S(1)} %bitcast.57, ...), channel_id=1, replica_groups=mesh['model'=4,'data'=32] {'model','data'}, use_global_device_ids=true, to_apply=%region_10.0 | all-reduce | flops 36 | bytes 288 | tf_op jit(solution)/shard_map/psum | solution.py:17
  587.8 1.6 multiply_subtract_fusion.3
  589.4 1.8 multiply_subtract_fusion.1
  591.2 1.7 multiply_subtract_fusion.2
  592.8 1.9 multiply_subtract_fusion
  (75 shorter events, 5.5 us)
Async XLA Ops:
  7.2 86.5 %reduce-scatter.11.cloned.1.call-start = ((), (), s32[]{:S(2)}) async-start(), calls=%async_computation.7 | async-start | bytes 2433024 | tf_op jit(solution)/shard_map/reduce_scatter | solution.py:31
  10.4 170.5 %reduce-scatter.7.cloned.1.call-start = ((), (), s32[]{:S(2)}) async-start(), calls=%async_computation.5 | async-start | bytes 4866048 | tf_op jit(solution)/shard_map/reduce_scatter | solution.py:31
  15.8 256.3 %reduce-scatter.9.cloned.1.call-start = ((), (), s32[]{:S(2)}) async-start(), calls=%async_computation.6 | async-start | bytes 7299072 | tf_op jit(solution)/shard_map/reduce_scatter | solution.py:31
  23.7 347.0 %reduce-scatter.5.cloned.1.call-start = ((), (), s32[]{:S(2)}) async-start(), calls=%async_computation.4 | async-start | bytes 9732096 | tf_op jit(solution)/shard_map/reduce_scatter | solution.py:31
  30.5 0.9 copy-start.3
  30.5 1.0 copy-start.2
  30.5 1.1 copy-start.1
  30.5 1.3 copy-start
  30.5 358.0 %copy-start.13 = (f32[9,24]{1,0:T(8,128)S(1)}, f32[9,24]{1,0:T(8,128)}, u32[]{:S(2)}) copy-start(f32[9,24]{1,0:T(8,128)} %param.26) | copy-start | bytes 2596
  30.5 358.1 %copy-start.18 = (f32[4,24]{1,0:T(4,128)S(1)}, f32[4,24]{1,0:T(4,128)}, u32[]{:S(2)}) copy-start(f32[4,24]{1,0:T(4,128)} %param.18) | copy-start | bytes 1156
  30.5 482.1 %copy-start.15 = (f32[2,768]{1,0:T(2,128)S(1)}, f32[2,768]{1,0:T(2,128)}, u32[]{:S(2)}) copy-start(f32[2,768]{1,0:T(2,128)} %param.22) | copy-start | bytes 18436
  30.6 482.2 %copy-start.16 = (f32[3,192]{1,0:T(4,128)S(1)}, f32[3,192]{1,0:T(4,128)}, u32[]{:S(2)}) copy-start(f32[3,192]{1,0:T(4,128)} %param.30) | copy-start | bytes 6916
  30.6 490.2 %copy-start.17 = (f32[3,24]{1,0:T(4,128)S(1)}, f32[3,24]{1,0:T(4,128)}, u32[]{:S(2)}) copy-start(f32[3,24]{1,0:T(4,128)} %param.31) | copy-start | bytes 868
  30.6 490.3 %copy-start.19 = (f32[2,24]{1,0:T(2,128)S(1)}, f32[2,24]{1,0:T(2,128)}, u32[]{:S(2)}) copy-start(f32[2,24]{1,0:T(2,128)} %param.23) | copy-start | bytes 580
  30.6 490.4 %copy-start.9 = (f32[9,192]{1,0:T(8,128)S(1)}, f32[9,192]{1,0:T(8,128)}, u32[]{:S(2)}) copy-start(f32[9,192]{1,0:T(8,128)} %param.27) | copy-start | bytes 20740
  30.6 490.4 %copy-start.11 = (f32[4,768]{1,0:T(4,128)S(1)}, f32[4,768]{1,0:T(4,128)}, u32[]{:S(2)}) copy-start(f32[4,768]{1,0:T(4,128)} %param.19) | copy-start | bytes 36868
  388.7 206.0 %copy-start.6 = (f32[9,24]{1,0:T(8,128)}, f32[9,24]{1,0:T(8,128)S(1)}, u32[]{:S(2)}) copy-start(f32[9,24]{1,0:T(8,128)S(1)} %get-tuple-element.45) | copy-start | bytes 2596
  388.8 205.9 %copy-start.14 = (f32[4,24]{1,0:T(4,128)}, f32[4,24]{1,0:T(4,128)S(1)}, u32[]{:S(2)}) copy-start(f32[4,24]{1,0:T(4,128)S(1)} %get-tuple-element.47) | copy-start | bytes 1156
  512.8 81.9 %copy-start.7 = (f32[2,768]{1,0:T(2,128)}, f32[2,768]{1,0:T(2,128)S(1)}, u32[]{:S(2)}) copy-start(f32[2,768]{1,0:T(2,128)S(1)} %get-tuple-element.43) | copy-start | bytes 18436
  512.9 81.8 %copy-start.10 = (f32[3,192]{1,0:T(4,128)}, f32[3,192]{1,0:T(4,128)S(1)}, u32[]{:S(2)}) copy-start(f32[3,192]{1,0:T(4,128)S(1)} %get-tuple-element.41) | copy-start | bytes 6916
  520.8 73.9 %copy-start.8 = (f32[3,24]{1,0:T(4,128)}, f32[3,24]{1,0:T(4,128)S(1)}, u32[]{:S(2)}) copy-start(f32[3,24]{1,0:T(4,128)S(1)} %multiply_add_fusion.9) | copy-start | bytes 868
  520.9 73.9 %copy-start.12 = (f32[2,24]{1,0:T(2,128)}, f32[2,24]{1,0:T(2,128)S(1)}, u32[]{:S(2)}) copy-start(f32[2,24]{1,0:T(2,128)S(1)} %multiply_add_fusion.11) | copy-start | bytes 580
  521.0 73.8 %copy-start.4 = (f32[9,192]{1,0:T(8,128)}, f32[9,192]{1,0:T(8,128)S(1)}, u32[]{:S(2)}) copy-start(f32[9,192]{1,0:T(8,128)S(1)} %multiply_add_fusion.4) | copy-start | bytes 20740
  521.1 73.7 %copy-start.5 = (f32[4,768]{1,0:T(4,128)}, f32[4,768]{1,0:T(4,128)S(1)}, u32[]{:S(2)}) copy-start(f32[4,768]{1,0:T(4,128)S(1)} %multiply_add_fusion.5) | copy-start | bytes 36868
Sparse Core Ops, SparseCore 0:
  11.5 82.1 reduce-scatter.10
  97.4 83.4 reduce-scatter.6
  184.7 87.3 reduce-scatter.8
  275.7 94.9 reduce-scatter.4
where the time goes:
time: 603 us; the launch traced here: 601 us
  waiting for transfers between devices  336 us (56%)
  blocking collectives  210 us (35%)
  other arithmetic  31.4 us (5%)
  between operations  14.1 us (2%)
  local copies, waits for them, and re-layouts  9.49 us (2%)
    reduce_scatter x4, waiting for transfers between devices, update_block(): lax.psum_scatter(grad_parts[0].astype(jnp.float32), 'data', scatter_dimen...  336 us
    psum x2, blocking collectives, update_block(): col_sum = lax.psum(jnp.sum(grad_sq, axis=1), row_axis)  132 us
    psum x1, blocking collectives, finish_update(): lax.psum(jnp.sum(update * update, axis=(1, 2), keepdims=True), ('model',...  62.1 us
    psum x1, blocking collectives, update_block(): row_sum = lax.psum(jnp.sum(grad_sq, axis=2), col_axis)  16.8 us
    convert_element_type x4, other arithmetic, update_block(): grad_parts[0].astype(jnp.float32)  14.4 us
  transfers between devices with their start and end apart: 4, of which 4 were waited for; matrix products, arithmetic and copies ran while one was open for 4% of the time, Pallas kernels for 0%

commit v1 on v0

v1 whole, which is shorter than its diff:
```python
import jax
import jax.numpy as jnp
from jax import lax
from jax.experimental import pallas as pl
from jax.experimental.pallas import tpu as pltpu
from jax.sharding import PartitionSpec as P

OPT_STEP = 4
EPS_SQ = 1e-30
BETA_TWO = 1.0 - OPT_STEP ** -0.8
LR_BASE = min(1e-2, OPT_STEP ** -0.5)

F32 = jnp.float32
FF = 3072.0
D = 768.0
MESH = pl.DeviceIdType.MESH
RANKS = 32
DIM = 768
THIN = 192
LANES = 128
SECOND = 1024
VEC = 1280
STEPS = 9
PLAIN = 4
HALF = 384
BLK = 24
MATS = 18
WIDE = 6
ROWCUT = (16, 8)

VEC_AT = tuple([(j, 0, DIM) for j in range(6)] + [(j, DIM, THIN) for j in range(8)] + [(j, SECOND, THIN) for j in range(4)])


def kernel(g_in, w_in, r_in, c_in, g_out, w_out, r_out, c_out, g_qkv, w_qkv, r_qkv, c_qkv, g_o, w_o, r_o, c_o,
           w_in_n, r_in_n, c_in_n, w_out_n, r_out_n, c_out_n, w_qkv_n, r_qkv_n, c_qkv_n, w_o_n, r_o_n, c_o_n,
           xin, s0, r0, r1, b2, r2, grad, gsm, pick_f, pick, vw_in, vw_out, vw_qkv, vw_o,
           vr_in, vc_in, vr_out, vc_out, vr_qkv, vc_qkv, vr_o, vc_o,
           square, dv_mom, mv_mom, dv_own, dv_got, mv_own, mv_got, mv_core, mv_rs, sc_own, sc_got, sc_core,
           ld_sem, sm_sem, d2d_s, d2d_r, p1_s, p1_r, p2_s, p2_r,
           dv_s, dv_r, mv_s, mv_r, sc_s, sc_r):
    d = lax.axis_index('data')
    x = lax.axis_index('model')
    core = lax.rem(d, 2)
    y = lax.rem(d // 2, 4)
    z = d // 8

    def at(axis, off):
        if axis == 'x':
            return {'model': lax.rem(x + off, 4)}
        if axis == 'y':
            return {'data': (z * 4 + lax.rem(y + off, 4)) * 2 + core}
        if axis == 'z':
            return {'data': (lax.rem(z + off, 4) * 4 + y) * 2 + core}
        return {'data': (z * 4 + y) * 2 + (1 - core)}

    loads = [pltpu.make_async_copy(g_in.at[k], xin.at[k], ld_sem.at[k]) for k in range(4)]
    loads += [pltpu.make_async_copy(g_out.at[k], xin.at[4 + k], ld_sem.at[4 + k]) for k in range(2)]
    loads += [pltpu.make_async_copy(g_qkv.at[pl.ds(DIM * k, DIM)], xin.at[6 + k], ld_sem.at[6 + k]) for k in range(2)]
    loads += [pltpu.make_async_copy(g_qkv.at[pl.ds(1536, THIN)], xin.at[8, pl.ds(0, THIN)], ld_sem.at[8]),
              pltpu.make_async_copy(g_o, xin.at[8, pl.ds(THIN, 576)], ld_sem.at[STEPS])]
    small = [(w_in, vw_in), (w_out, vw_out), (w_qkv, vw_qkv), (w_o, vw_o), (r_in, vr_in), (c_in, vc_in),
             (r_out, vr_out), (c_out, vc_out), (r_qkv, vr_qkv), (c_qkv, vc_qkv), (r_o, vr_o), (c_o, vc_o)]
    small = [pltpu.make_async_copy(s, t, sm_sem.at[j]) for j, (s, t) in enumerate(small)]
    for cp in loads + small:
        cp.start()

    barrier = pltpu.get_barrier_semaphore()
    peers = [at('c', 1)] + [at(a, j) for a in ('y', 'z', 'x') for j in (1, 2, 3)]
    for p in peers:
        pl.semaphore_signal(barrier, inc=1, device_id=p, device_id_type=MESH)

    for side in range(2):
        cc = (1 - core) if side == 0 else core
        row = lax.broadcasted_iota(jnp.int32, (BLK, HALF), 0)
        col = lax.broadcasted_iota(jnp.int32, (BLK, HALF), 1)
        for b in range(8):
            pick_f[pl.ds(BLK * b, BLK)] = jnp.where(col == row + 48 * b + 24 * cc, 1.0, 0.0)
        pick[side] = pick_f[...].astype(jnp.bfloat16)

    pl.semaphore_wait(barrier, len(peers))

    def remote(src, dst, ss, rs, dev):
        return pltpu.make_async_remote_copy(src_ref=src, dst_ref=dst, send_sem=ss, recv_sem=rs,
                                            device_id=dev, device_id_type=MESH)

    def d2d(k, h):
        return remote(s0.at[k, h], r0.at[k, h], d2d_s.at[k, h], d2d_r.at[k, h], at('c', 1))

    def part(k, side, fn):
        @pl.when(k < PLAIN)
        def _():
            def group(g, carry):
                v = xin[k, pl.ds(pl.multiple_of(48 * g, 16), 48), :].astype(F32)
                first = (core == 0) if side == 1 else (core == 1)
                v = jnp.where(first, v[:BLK], v[BLK:])
                for h in range(2):
                    fn(h, pl.ds(g // 4, 1), pl.ds(lax.rem(g, 4), 1), v[:, HALF * h:HALF * (h + 1)].reshape(1, 1, BLK, HALF))
                return carry
            lax.fori_loop(0, 16, group, 0)

        @pl.when(k >= PLAIN)
        def _():
            def group(g, carry):
                for h in range(2):
                    v = xin[k, pl.ds(HALF * h, HALF), pl.ds(pl.multiple_of(HALF * g, LANES), HALF)]
                    v = lax.dot_general(pick[side], v, (((1,), (1,)), ((), ())), preferred_element_type=F32)
                    fn(h, pl.ds(2 * g, 2), slice(None), v.reshape(2, 4, BLK, HALF))
                return carry
            lax.fori_loop(0, 2, group, 0)

    def stage0(k):
        for j in range(STEPS):
            @pl.when(k == j)
            def _(j=j):
                loads[j].wait()
                if j == 8:
                    loads[STEPS].wait()

        def put(h, zs, ys, v):
            s0[k, h, zs, ys] = v
        part(k, 0, put)
        for h in range(2):
            d2d(k, h).start()

    def ring(h, first):
        axis = ('y', 'z')[h] if first else ('z', 'y')[h]
        return axis, (y if axis == 'y' else z)

    def src1(k, h, t, s):
        return r0.at[k, 0, pl.ds(2 * s, 2), t] if h == 0 else r0.at[k, 1, t, pl.ds(2 * s, 2)]

    def cut(h, s):
        return pl.ds(0, ROWCUT[h]) if s == 0 else pl.ds(ROWCUT[h], BLK - ROWCUT[h])

    def src2(k, h, t, s):
        return b2.at[k, h, t, cut(h, s)]

    def mod4(v):
        return lax.rem(v + 8, 4)

    PLAN = ((-2, 0), (-1, 1), (-1, 0), (2, 1), (1, 0), (1, 1))

    def msg(first, k, h, m):
        axis, n = ring(h, first)
        off, s = PLAN[m]
        t = mod4(n + off)
        dev = at(axis, 3 if m < 3 else 1)
        if first:
            return remote(src1(k, h, t, s), r1.at[k, h, m], p1_s.at[k, h, m], p1_r.at[k, h, m], dev)
        rows = ROWCUT[h] if s == 0 else BLK - ROWCUT[h]
        return remote(src2(k, h, t, s), r2.at[k, h, m, pl.ds(0, rows)], p2_s.at[k, h, m], p2_r.at[k, h, m], dev)

    def got(first, k, h, m):
        if first:
            return r1[k, h, m]
        s = PLAN[m][1]
        return r2[k, h, m, pl.ds(0, ROWCUT[h] if s == 0 else BLK - ROWCUT[h])]

    def send_raw(first, k, h):
        for m in (0, 3, 1, 4):
            msg(first, k, h, m).start()

    def stage1(k):
        for h in range(2):
            d2d(k, h).wait_recv()

        def add(h, zs, ys, v):
            r0[k, h, zs, ys] += v
        part(k, 1, add)
        for h in range(2):
            send_raw(True, k, h)

    def relay(first, k):
        for h in range(2):
            n = ring(h, first)[1]
            for m_in, m_out in ((0, 2), (3, 5)):
                msg(first, k, h, m_in).wait_recv()
                off, s = PLAN[m_out]
                ref = (src1 if first else src2)(k, h, mod4(n + off), s)
                ref[...] += got(first, k, h, m_in)
                msg(first, k, h, m_out).start()

    def stage3(k):
        for h in range(2):
            n = ring(h, True)[1]
            for s, left, right in ((0, 2, 4), (1, 1, 5)):
                msg(True, k, h, left).wait_recv()
                msg(True, k, h, right).wait_recv()
                b2[k, h, pl.ds(2 * s, 2)] = src1(k, h, n, s)[...] + got(True, k, h, left) + got(True, k, h, right)
            send_raw(False, k, h)

    def stage5(k):
        for h in range(2):
            n = ring(h, False)[1]
            for s, left, right in ((0, 2, 4), (1, 1, 5)):
                msg(False, k, h, left).wait_recv()
                msg(False, k, h, right).wait_recv()
                total = src2(k, h, n, s)[...] + got(False, k, h, left) + got(False, k, h, right)
                grad[k, cut(h, s), pl.ds(HALF * h, HALF)] = total / RANKS

    lane = lax.broadcasted_iota(jnp.int32, (1, LANES), 1)

    def put_lane(vec, j, value):
        return jnp.where(lane == j, value, vec)

    def prepare():
        for cp in small:
            cp.wait()
        square[...] = jnp.zeros_like(square)
        square[0:4, 0:BLK] = vr_in[...]
        square[4:6, 0:BLK] = vc_out[...]
        square[6:15, 0:BLK] = vr_qkv[...]
        square[15:18, 0:BLK] = vc_o[...]
        dv_mom[...] = square[...].T[0:BLK]
        mv_mom[...] = jnp.ones_like(mv_mom)
        mv_mom[0:4, 0:DIM] = vc_in[...]
        mv_mom[4:6, 0:DIM] = vr_out[...]
        mv_mom[0:8, DIM:960] = vc_qkv[0:8]
        mv_mom[0:1, SECOND:1216] = vc_qkv[8:STEPS]
        mv_mom[1:4, SECOND:1216] = vr_o[...]
        mv_own[...] = jnp.zeros_like(mv_own)
        sc_own[...] = jnp.zeros_like(sc_own)
        vec = jnp.zeros((1, LANES), F32)
        for j in range(MATS):
            w = weight_of(j)
            vec = put_lane(vec, j, jnp.sum(jnp.sum(w * w, axis=0, keepdims=True), axis=1, keepdims=True))
        sc_own[2:3] = vec

    def weight_of(j):
        return vw_in[j] if j < 4 else vw_out[j - 4] if j < 6 else vw_qkv[j - 6] if j < 15 else vw_o[j - 15]

    def grad_of(j):
        return grad[j] if j < WIDE else gsm[j - WIDE]


    def trip(i, carry):
        for lag, stage in enumerate((stage0, stage1, lambda k: relay(True, k), stage3, lambda k: relay(False, k), stage5)):
            @pl.when(jnp.logical_and(i >= lag, i < STEPS + lag))
            def _(lag=lag, stage=stage):
                stage(i - lag)

        @pl.when(i == 5)
        def _():
            prepare()
        return carry
    lax.fori_loop(0, STEPS + 5, trip, 0)

    for j in range(12):
        k, q = 6 + j // 4, j % 4
        if q % 2 == 0:
            gsm[j] = grad[k, :, THIN * q:THIN * q + THIN]
        else:
            gsm[j] = pltpu.roll(grad[k, :, THIN * q - 64:THIN * q + THIN], THIN, 1)[:, :THIN]

    dv = jnp.zeros((BLK, LANES), F32)
    for j in range(MATS):
        g = grad_of(j)
        s = g * g + EPS_SQ
        dv = jnp.where(lane == j, jnp.sum(s, axis=1, keepdims=True), dv)
        row, at_lane, width = VEC_AT[j]
        mv_own[row:row + 1, at_lane:at_lane + width] = jnp.sum(s, axis=0, keepdims=True)
    dv_own[...] = dv

    def spread(axis, src, dst, ss, rs):
        return [remote(src, dst.at[j], ss.at[j], rs.at[j], at(axis, j)) for j in (1, 2, 3)]

    def collect(src, dst, copies):
        for cp in copies:
            cp.wait_recv()
        return (src[...] + dst[2]) + (dst[1] + dst[3])

    dv_cp = spread('x', dv_own, dv_got, dv_s, dv_r)
    for cp in dv_cp:
        cp.start()
    core_cp = remote(mv_own, mv_core.at[0], mv_s.at[0, 0], mv_r.at[0, 0], at('c', 1))
    core_cp.start()
    core_cp.wait_recv()
    mv_core[1] = mv_own[...] + mv_core[0]
    y_cp = spread('y', mv_core.at[1], mv_got.at[0], mv_s.at[1], mv_r.at[1])
    for cp in y_cp:
        cp.start()
    count = jnp.where(lane < WIDE, FF, D)
    dv_new = BETA_TWO * dv_mom[...] + (1.0 - BETA_TWO) * (collect(dv_own, dv_got, dv_cp) / count)
    dv_inv = 1.0 / jnp.sqrt(jnp.where(lane < MATS, dv_new, 1.0))
    square[0:BLK] = dv_new
    turned = square[...].T
    r_in_n[...] = turned[0:4, 0:BLK]
    c_out_n[...] = turned[4:6, 0:BLK]
    r_qkv_n[...] = turned[6:15, 0:BLK]
    c_o_n[...] = turned[15:18, 0:BLK]
    for j in range(MATS):
        g = grad_of(j) * dv_inv[:, j:j + 1]
        if j < WIDE:
            grad[j] = g
        else:
            gsm[j - WIDE] = g
    mv_core[2] = collect(mv_core.at[1], mv_got.at[0], y_cp)
    z_cp = spread('z', mv_core.at[2], mv_got.at[1], mv_s.at[2], mv_r.at[2])
    for cp in z_cp:
        cp.start()
    mv_sum = collect(mv_core.at[2], mv_got.at[1], z_cp)
    mv_new = BETA_TWO * mv_mom[...] + (1.0 - BETA_TWO) * (mv_sum / D)
    mv_mom[...] = mv_new
    c_in_n[...] = mv_mom[0:4, 0:DIM]
    r_out_n[...] = mv_mom[4:6, 0:DIM]
    c_qkv_n[0:8] = mv_mom[0:8, DIM:960]
    c_qkv_n[8:STEPS] = mv_mom[0:1, SECOND:1216]
    r_o_n[...] = mv_mom[1:4, SECOND:1216]
    mv_inv = 1.0 / jnp.sqrt(mv_new)
    mv_rs[...] = mv_inv

    upd_vec = jnp.zeros((1, LANES), F32)
    row_vec = jnp.sum(dv_new, axis=0, keepdims=True) / 4
    for j in range(MATS):
        row, at_lane, width = VEC_AT[j]
        u = grad_of(j) * mv_rs[row:row + 1, at_lane:at_lane + width]
        if j < WIDE:
            grad[j] = u
        else:
            gsm[j - WIDE] = u
        upd_vec = put_lane(upd_vec, j, jnp.sum(jnp.sum(u * u, axis=0, keepdims=True), axis=1, keepdims=True))
        if 4 <= j < 6 or j >= 15:
            row_vec = put_lane(row_vec, j, jnp.sum(mv_mom[row:row + 1, at_lane:at_lane + width], axis=1, keepdims=True) / 32)
    sc_own[0:1] = upd_vec
    sc_own[1:2] = row_vec

    core_sc = remote(sc_own, sc_core.at[0], sc_s.at[0, 0], sc_r.at[0, 0], at('c', 1))
    core_sc.start()
    core_sc.wait_recv()
    sc_core[1] = sc_own[...] + sc_core[0]
    sc_cp = []
    for n, axis in enumerate(('y', 'z', 'x')):
        cps = spread(axis, sc_core.at[n + 1], sc_got.at[n], sc_s.at[n + 1], sc_r.at[n + 1])
        for cp in cps:
            cp.start()
        sc_cp += cps
        sc_core[n + 2] = collect(sc_core.at[n + 1], sc_got.at[n], cps)
    full = jnp.where(lane < WIDE, FF * D, D * D)
    rows = jnp.where(jnp.logical_and(lane >= 4, lane < 6), FF, D)
    row_mean = sc_core[4, 1:2] / rows
    upd_rms = jnp.sqrt(row_mean * (sc_core[4, 0:1] / full))
    w_rms = jnp.sqrt(sc_core[4, 2:3] / full)
    scale = LR_BASE * jnp.maximum(1e-3, w_rms) * (jnp.sqrt(row_mean) / jnp.maximum(1.0, upd_rms))
    for j in range(MATS):
        new = weight_of(j) - scale[:, j:j + 1] * grad_of(j)
        if j < 4:
            w_in_n[j] = new
        elif j < 6:
            w_out_n[j - 4] = new
        elif j < 15:
            w_qkv_n[j - 6] = new
        else:
            w_o_n[j - 15] = new

    def drain(k, carry):
        for h in range(2):
            d2d(k, h).wait_send()
            for m in range(6):
                msg(True, k, h, m).wait_send()
                msg(False, k, h, m).wait_send()
        return carry
    lax.fori_loop(0, STEPS, drain, 0)
    for cp in dv_cp + [core_cp] + y_cp + z_cp + [core_sc] + sc_cp:
        cp.wait_send()


def write_out(*refs):
    n = len(refs) // 2
    copies = [pltpu.make_async_copy(refs[j], refs[n + j], refs[-1].at[j]) for j in range(n)]
    for cp in copies:
        cp.start()
    for cp in copies:
        cp.wait()


def solution(mesh):
    rows_data = (P('data', None, None, 'model'), P(None, 'data', 'model'), P(None, 'data'), P(None, 'model'))
    rows_model = (P('data', None, 'model', None), P(None, 'model', 'data'), P(None, 'model'), P(None, 'data'))
    DMA = pltpu.SemaphoreType.DMA

    def step_all(grad_in, w_in, row_in, col_in, grad_out, w_out, row_out, col_out,
                 grad_qkv, w_qkv, row_qkv, col_qkv, grad_o, w_o, row_o, col_o):
        args = (grad_in[0], w_in, row_in, col_in,
                grad_out[0], w_out.swapaxes(1, 2), row_out, col_out,
                grad_qkv[0].swapaxes(1, 2).reshape(1728, DIM), w_qkv, row_qkv, col_qkv,
                grad_o[0].reshape(576, DIM), w_o.swapaxes(1, 2), row_o, col_o)
        small = [a for n, a in enumerate(args) if n % 4]
        outs = [jax.ShapeDtypeStruct(a.shape, a.dtype) for a in small]
        held = [pltpu.VMEM(a.shape, a.dtype) for a in small]
        vm = lambda *s: pltpu.VMEM(s, F32)
        res = pl.pallas_call(
            kernel,
            out_shape=held,
            in_specs=[pl.BlockSpec(memory_space=pl.ANY)] * len(args),
            out_specs=[pl.BlockSpec(memory_space=pltpu.VMEM)] * len(outs),
            scratch_shapes=[
                pltpu.VMEM((STEPS, DIM, DIM), jnp.bfloat16),
                vm(STEPS, 2, 4, 4, BLK, HALF), vm(STEPS, 2, 4, 4, BLK, HALF),
                vm(STEPS, 2, 6, 2, BLK, HALF), vm(STEPS, 2, 4, BLK, HALF), vm(STEPS, 2, 6, 16, HALF),
                vm(STEPS, BLK, DIM), vm(12, BLK, THIN),
                vm(THIN, HALF), pltpu.VMEM((2, THIN, HALF), jnp.bfloat16),
                vm(4, BLK, DIM), vm(2, BLK, DIM), vm(STEPS, BLK, THIN), vm(3, BLK, THIN),
                vm(4, BLK), vm(4, DIM), vm(2, DIM), vm(2, BLK), vm(STEPS, BLK), vm(STEPS, THIN), vm(3, THIN), vm(3, BLK),
                vm(LANES, LANES), vm(BLK, LANES), vm(8, VEC),
                vm(BLK, LANES), vm(4, BLK, LANES), vm(8, VEC), vm(2, 4, 8, VEC), vm(3, 8, VEC), vm(8, VEC),
                vm(8, LANES), vm(3, 4, 8, LANES), vm(5, 8, LANES),
                DMA((10,)), DMA((12,)), DMA((STEPS, 2)), DMA((STEPS, 2)),
                DMA((STEPS, 2, 6)), DMA((STEPS, 2, 6)), DMA((STEPS, 2, 6)), DMA((STEPS, 2, 6)),
                DMA((4,)), DMA((4,)), DMA((3, 4)), DMA((3, 4)), DMA((4, 4)), DMA((4, 4)),
            ],
            compiler_params=pltpu.CompilerParams(
                collective_id=0, has_side_effects=True, vmem_limit_bytes=58_000_000),
            name='adafactor',
        )(*args)
        res = list(pl.pallas_call(
            write_out,
            out_shape=outs,
            in_specs=[pl.BlockSpec(memory_space=pltpu.VMEM)] * len(outs),
            out_specs=[pl.BlockSpec(memory_space=pl.ANY)] * len(outs),
            scratch_shapes=[DMA((len(outs),))],
            name='write_out',
        )(*[pltpu.with_memory_space_constraint(r, pltpu.VMEM) for r in res]))
        for n in (3, STEPS):
            res[n] = res[n].swapaxes(1, 2)
        return tuple(res)

    in_specs = rows_data + rows_model + rows_data + rows_model
    out_specs = rows_data[1:] + rows_model[1:] + rows_data[1:] + rows_model[1:]
    return jax.shard_map(step_all, mesh=mesh, in_specs=in_specs, out_specs=out_specs, check_vma=False)
```

time: 603 us -> 98.4 us (0.16)
  waiting for transfers between devices: 336 us -> 0 us
  blocking collectives: 210 us -> 0 us
  Pallas kernels: 0 us -> 97.7 us
  other arithmetic: 31.4 us -> 0 us
  between operations: 14.1 us -> 0.66 us
  local copies, waits for them, and re-layouts: 9.49 us -> 0 us
    reduce_scatter x4 -> x0, waiting for transfers between devices: 336 us -> none  [update_block(): lax.psum_scatter(grad_parts[0].astype(jnp.float32), 'data', scatter_dimen...]
    psum x4 -> x0, blocking collectives: 210 us -> none  [the longest x2 132 us: update_block(): col_sum = lax.psum(jnp.sum(grad_sq, axis=1), row_axis)]
    pallas_call x0 -> x2, Pallas kernels: none -> 97.7 us  [the longest x1 96.7 us: step_all(): pl.pallas_call(kernel, out_shape=held, in_specs=[pl.BlockSpec(memory_spac...]
    convert_element_type x4 -> x0, other arithmetic: 14.4 us -> none  [update_block(): grad_parts[0].astype(jnp.float32)]
    reduce_sum x16 -> x0, other arithmetic: 9.67 us -> none  [the longest x4 4.53 us: finish_update(): jnp.sum(update * update, axis=(1, 2), keepdims=True)]
    unnamed x43 -> x0, local copies, waits for them, and re-layouts: 9.49 us -> none
    sub x4 -> x0, other arithmetic: 6.91 us -> none  [finish_update(): weight - LR_BASE * jnp.maximum(0.001, w_rms) * update]
  transfers between devices with their start and end apart: 4 -> 0, of which waited for: 4 -> 0; matrix products, arithmetic and copies ran while one was open for 4% -> 0% of each run, Pallas kernels for 0% -> 0%
where the time goes in v1:
time: 98.4 us; the launch traced here: 98.3 us
  Pallas kernels  97.7 us (99%)
    pallas_call x1, Pallas kernels, step_all(): pl.pallas_call(kernel, out_shape=held, in_specs=[pl.BlockSpec(memory_spac...  96.7 us

profile of v1, /device:TPU:0, one launch (start us, length us, event | category | flops | bytes accessed | tf_op | source)
XLA Modules:
  0.0 98.3 jit_solution(17119781259762447405)
XLA Ops:
  0.7 96.7 %adafactor.1 = (f32[4,24,768]{2,1,0:T(8,128)S(1)}, f32[4,24]{1,0:T(4,128)S(1)}, f32[4,768]{1,0:T(4,128)S(1)}, f32[2,24,768]{2,1,0:T(8,128)S(1)}, f32[2,768]{1,0:...) custom-call(bf16[4,768,768]{2,1,0:T(8,128)(2,1)} %bitcast.12, ...), custom_call_target="tpu_custom_call" | custom-call | tf_op jit(solution)/shard_map/adafactor/pallas_call | solution.py:391
  97.3 1.0 %write_out.1 = (f32[4,24,768]{2,1,0:T(8,128)}, f32[4,24]{1,0:T(4,128)}, f32[4,768]{1,0:T(4,128)}, f32[2,24,768]{2,1,0:T(8,128)}, f32[2,768]{1,0:T(2,128)}, /*ind...) custom-call(f32[4,24,768]{2,1,0:T(8,128)S(1)} %get-tuple-element.36., ...), custom_call_target="tpu_custom_call" | custom-call | tf_op jit(solution)/shard_map/write_out/pallas_call | solution.py:415

commit v2 on v0

v2 whole, which is shorter than its diff:
```python
import jax
import jax.numpy as jnp
from jax import lax
from jax.experimental import pallas as pl
from jax.experimental.pallas import tpu as pltpu
from jax.sharding import PartitionSpec as P

OPT_STEP = 4
EPS_SQ = 1e-30
BETA_TWO = 1.0 - OPT_STEP ** -0.8
LR_BASE = min(1e-2, OPT_STEP ** -0.5)

F32 = jnp.float32
MESH = pl.DeviceIdType.MESH
FF, D = 3072.0, 768.0
DIM = 768
THIN = 192
LANES = 128
PAIR = 256
SLABS = 9
PLAIN = 4
WIDE = 6
MATS = 18
CUTS = 1
STEPS = SLABS * CUTS
HALF = 384
CW = HALF // CUTS
BLK = 24
ROWCUT = (16, 8)
UP = 2.0 ** 48

LAG_ADD, LAG_RELAY1, LAG_TURN, LAG_RELAY2, LAG_SUM = 1, 2, 3, 4, 5
LAG_DV, LAG_CORE, LAG_Y, LAG_Z = 6, 7, 8, 9


def mod4(v):
    return lax.rem(v + 8, 4)


def cut(h, s):
    return pl.ds(0, ROWCUT[h]) if s == 0 else pl.ds(ROWCUT[h], BLK - ROWCUT[h])


def kernel(g_in, w_in, r_in, c_in, g_out, w_out, r_out, c_out, g_qkv, w_qkv, r_qkv, c_qkv, g_o, w_o, r_o, c_o,
           w_in_n, r_in_n, c_in_n, w_out_n, r_out_n, c_out_n, w_qkv_n, r_qkv_n, c_qkv_n, w_o_n, r_o_n, c_o_n,
           xin, s0, r0, r1a, r1b, b2, r2a, r2b, grad, gsm, pick_f, pick, vw_in, vw_out, vw_qkv, vw_o,
           vr_in, vc_in, vr_out, vc_out, vr_qkv, vc_qkv, vr_o, vc_o,
           square, thin_a, thin_b, dv_mom, dv_all, dv_own, dv_got, mv_mom, mv_new, mv_own, mv_core, mv_one, mv_y, mv_two, mv_z,
           sc_own, sc_got, ld_sem, sm_sem, d2d_s, d2d_r, p1_s, p1_r, p2_s, p2_r, dv_s, dv_r, mv_s, mv_r, sc_s, sc_r):
    d = lax.axis_index('data')
    x = lax.axis_index('model')
    core = lax.rem(d, 2)
    y = lax.rem(d // 2, 4)
    z = d // 8

    def at(axis, off):
        if axis == 'x':
            return {'model': lax.rem(x + off, 4)}
        if axis == 'y':
            return {'data': (z * 4 + lax.rem(y + off, 4)) * 2 + core}
        if axis == 'z':
            return {'data': (lax.rem(z + off, 4) * 4 + y) * 2 + core}
        return {'data': (z * 4 + y) * 2 + (1 - core)}

    def local(src, dst, sem):
        return pltpu.make_async_copy(src, dst, sem)

    loads = [local(g_in.at[k], xin.at[k], ld_sem.at[k]) for k in range(PLAIN)]
    loads += [local(g_out.at[k - PLAIN], xin.at[k], ld_sem.at[k]) for k in range(PLAIN, WIDE)]
    loads += [local(g_qkv.at[pl.ds(DIM * k, DIM)], xin.at[WIDE + k], ld_sem.at[WIDE + k]) for k in range(2)]
    loads += [local(g_qkv.at[pl.ds(2 * DIM, THIN)], xin.at[SLABS - 1, pl.ds(0, THIN)], ld_sem.at[SLABS - 1]),
              local(g_o, xin.at[SLABS - 1, pl.ds(THIN, DIM - THIN)], ld_sem.at[SLABS])]
    small = [(w_in, vw_in), (w_out, vw_out), (w_qkv, vw_qkv), (w_o, vw_o), (r_in, vr_in), (c_in, vc_in),
             (r_out, vr_out), (c_out, vc_out), (r_qkv, vr_qkv), (c_qkv, vc_qkv), (r_o, vr_o), (c_o, vc_o)]
    small = [local(s, t, sm_sem.at[j]) for j, (s, t) in enumerate(small)]
    for cp in loads + small:
        cp.start()

    barrier = pltpu.get_barrier_semaphore()
    peers = [at('c', 1)] + [at(a, j) for a in 'yzx' for j in (1, 2, 3)]
    for p in peers:
        pl.semaphore_signal(barrier, inc=1, device_id=p, device_id_type=MESH)
    pl.semaphore_wait(barrier, len(peers))

    def remote(src, dst, ss, rs, dev):
        return pltpu.make_async_remote_copy(src_ref=src, dst_ref=dst, send_sem=ss, recv_sem=rs,
                                            device_id=dev, device_id_type=MESH)

    def d2d(s, h):
        return remote(s0.at[s, h], r0.at[s, h], d2d_s.at[s, h], d2d_r.at[s, h], at('c', 1))

    def make_pick():
        for side in range(2):
            cc = (1 - core) if side == 0 else core
            row = lax.broadcasted_iota(jnp.int32, (BLK, HALF), 0)
            col = lax.broadcasted_iota(jnp.int32, (BLK, HALF), 1)
            for b in range(8):
                pick_f[pl.ds(BLK * b, BLK)] = jnp.where(col == row + 2 * BLK * b + BLK * cc, 1.0, 0.0)
            pick[side] = pick_f[...].astype(jnp.bfloat16)

    def part(s, side, fn):
        k = s // CUTS
        start = CW * lax.rem(s, CUTS)

        @pl.when(k < PLAIN)
        def _():
            first = (core == 0) if side == 1 else (core == 1)
            for g in range(16):
                for h in range(2):
                    v = xin[k, pl.ds(2 * BLK * g, 2 * BLK), pl.ds(pl.multiple_of(start + HALF * h, LANES), CW)].astype(F32)
                    fn(h, pl.ds(g // 4, 1), pl.ds(g % 4, 1), jnp.where(first, v[:BLK], v[BLK:]).reshape(1, 1, BLK, CW))

        @pl.when(k >= PLAIN)
        def _():
            for g in range(2):
                for h in range(2):
                    v = xin[k, pl.ds(pl.multiple_of(start + HALF * h, LANES), CW), pl.ds(HALF * g, HALF)]
                    v = lax.dot_general(pick[side], v, (((1,), (1,)), ((), ())), preferred_element_type=F32)
                    fn(h, pl.ds(2 * g, 2), slice(None), v.reshape(2, 4, BLK, CW))

    def stage_split(s):
        for j in range(SLABS):
            @pl.when(s == j * CUTS)
            def _(j=j):
                loads[j].wait()
                if j == SLABS - 1:
                    loads[SLABS].wait()

        def put(h, zs, ys, v):
            s0[s, h, zs, ys] = v
        part(s, 0, put)
        for h in range(2):
            d2d(s, h).start()

    def ring(h, first):
        axis = ('y', 'z')[h] if first else ('z', 'y')[h]
        return axis, (y if axis == 'y' else z)

    def block(first, s, h, t, piece):
        if not first:
            return b2.at[s, h, t, cut(h, piece)]
        return r0.at[s, 0, pl.ds(2 * piece, 2), t] if h == 0 else r0.at[s, 1, t, pl.ds(2 * piece, 2)]

    def landing(first, h, piece):
        return pl.ds(2 * piece, 2) if first else cut(h, piece)

    PLAN = ((-2, 0, 0), (2, 1, 1), (-1, 1, 0), (1, 0, 1), (-1, 0, 0), (1, 1, 1))

    def msg(first, s, h, m):
        axis, n = ring(h, first)
        off, piece, way = PLAN[m]
        send, recv, relayed, landed = (p1_s, p1_r, r1a, r1b) if first else (p2_s, p2_r, r2a, r2b)
        src = block(first, s, h, mod4(n + off), piece)
        if m < 2:
            dst = relayed.at[s, h, way] if first else relayed.at[s, h, way, pl.ds(0, cut(h, piece).size)]
        else:
            dst = landed.at[s, h, way, landing(first, h, piece)]
        return remote(src, dst, send.at[s, h], recv.at[s, h, min(m, 2)], at(axis, 1 if way else 3))

    def send_raw(first, s, h):
        for m in range(4):
            msg(first, s, h, m).start()

    def stage_add(s):
        for h in range(2):
            d2d(s, h).wait_recv()

        def add(h, zs, ys, v):
            r0[s, h, zs, ys] += v
        part(s, 1, add)
        for h in range(2):
            send_raw(True, s, h)

    def relay(first, s):
        for h in range(2):
            n = ring(h, first)[1]
            for m in range(2):
                msg(first, s, h, m).wait_recv()
                off, piece, way = PLAN[4 + m]
                ref = block(first, s, h, mod4(n + off), piece)
                if first:
                    ref[...] += r1a[s, h, way]
                else:
                    ref[...] += r2a[s, h, way, pl.ds(0, cut(h, piece).size)]
                msg(first, s, h, 4 + m).start()

    def wait_landed(first, s, h):
        landed, recv = (r1b, p1_r) if first else (r2b, p2_r)
        local(landed.at[s, h], landed.at[s, h], recv.at[s, h, 2]).wait()

    def stage_turn(s):
        for h in range(2):
            n = ring(h, True)[1]
            wait_landed(True, s, h)
            own = r0[s, 0, :, n] if h == 0 else r0[s, 1, n]
            b2[s, h] = own + r1b[s, h, 0] + r1b[s, h, 1]
            send_raw(False, s, h)

    def stage_sum(s):
        k = s // CUTS
        start = CW * lax.rem(s, CUTS)
        for h in range(2):
            n = ring(h, False)[1]
            wait_landed(False, s, h)
            total = b2[s, h, n] + r2b[s, h, 0] + r2b[s, h, 1]
            grad[k, :, pl.ds(pl.multiple_of(start + HALF * h, LANES), CW)] = total / 32

    lane = lax.broadcasted_iota(jnp.int32, (1, LANES), 1)
    col = lax.broadcasted_iota(jnp.int32, (1, DIM), 1)
    count = jnp.where(lane < WIDE, FF, D)

    def of_mat(q):
        return jnp.logical_and(col >= THIN * q, col < THIN * q + THIN)

    def total(v):
        return jnp.sum(jnp.sum(v, axis=0, keepdims=True), axis=1, keepdims=True)

    def weight_of(j):
        return vw_in[j] if j < 4 else vw_out[j - 4] if j < 6 else vw_qkv[j - 6] if j < 15 else vw_o[j - 15]

    def prepare():
        for cp in small:
            cp.wait()
        make_pick()
        square[...] = jnp.zeros_like(square)
        square[0:4, 0:BLK] = vr_in[...]
        square[4:6, 0:BLK] = vc_out[...]
        square[6:15, 0:BLK] = vr_qkv[...]
        square[15:18, 0:BLK] = vc_o[...]
        dv_mom[...] = square[...].T[0:BLK]
        thin_a[...] = jnp.zeros_like(thin_a)
        thin_a[0:9, 0:THIN] = vc_qkv[...]
        thin_a[9:12, 0:THIN] = vr_o[...]
        thin_b[...] = pltpu.roll(thin_a[...], 64, 1)
        for k in range(4):
            mv_mom[k] = vc_in[k:k + 1]
        for k in range(2):
            mv_mom[4 + k] = vr_out[k:k + 1]
        for j in range(12):
            k, q = WIDE + j // 4, j % 4
            if q % 2 == 0:
                mv_mom[k, :, THIN * q:THIN * q + THIN] = thin_a[j:j + 1, 0:THIN]
            else:
                span = slice(THIN * q - 64, THIN * q + THIN)
                mv_mom[k, :, span] = jnp.where(col[:, :PAIR] < 64, mv_mom[k, :, span], thin_b[j:j + 1])
        mv_own[...] = jnp.zeros_like(mv_own)
        sc_own[...] = jnp.zeros_like(sc_own)
        dv_all[...] = jnp.ones_like(dv_all)
        vec = jnp.zeros((1, LANES), F32)
        for j in range(MATS):
            w = weight_of(j)
            vec = jnp.where(lane == j, total(w * w), vec)
        mv_own[SLABS - 1, 2:3, LANES:PAIR] = vec

    def spread(axis, src, dst, ss, rs):
        return [remote(src, dst.at[j], ss.at[j], rs.at[j], at(axis, j)) for j in (1, 2, 3)]

    def start(copies):
        for cp in copies:
            cp.start()

    def collect(src, dst, copies):
        for cp in copies:
            cp.wait_recv()
        return (src[...] + dst[2]) + (dst[1] + dst[3])

    def dv_copies(k):
        return spread('x', dv_own.at[k], dv_got.at[k], dv_s.at[k], dv_r.at[k])

    def core_copy(k):
        return remote(mv_own.at[k], mv_core.at[k], mv_s.at[0, k, 0], mv_r.at[0, k, 0], at('c', 1))

    def y_copies(k):
        return spread('y', mv_one.at[k], mv_y.at[k], mv_s.at[1, k], mv_r.at[1, k])

    def z_copies(k):
        return spread('z', mv_two.at[k], mv_z.at[k], mv_s.at[2, k], mv_r.at[2, k])

    def sums(k):
        g = grad[k]
        s = g * g + EPS_SQ
        mv_own[k, 0:1] = jnp.sum(s, axis=0, keepdims=True)

        @pl.when(k < WIDE)
        def _():
            dv_own[k] = jnp.where(lane == k, jnp.sum(s, axis=1, keepdims=True), 0.0)

        @pl.when(k >= WIDE)
        def _():
            dv = jnp.zeros((BLK, LANES), F32)
            for q in range(4):
                dv = jnp.where(lane == 4 * k - 18 + q, jnp.sum(jnp.where(of_mat(q), s, 0.0), axis=1, keepdims=True), dv)
            dv_own[k] = dv
        start(dv_copies(k))

    def mats_of(k):
        low = jnp.where(k < WIDE, k, 4 * k - 18)
        return jnp.logical_and(lane >= low, lane < jnp.where(k < WIDE, k + 1, 4 * k - 14))

    def data_side(k):
        mine = mats_of(k)
        new = BETA_TWO * dv_mom[...] + (1.0 - BETA_TWO) * (collect(dv_own.at[k], dv_got.at[k], dv_copies(k)) / count)
        dv_all[...] = jnp.where(mine, new, dv_all[...])
        mv_own[k, 2:3, 0:LANES] = jnp.where(mine, jnp.sum(new, axis=0, keepdims=True), 0.0)
        inv = 1.0 / jnp.sqrt(jnp.where(mine, new, 1.0))

        def column(j):
            return jnp.sum(jnp.where(lane == j, inv, 0.0), axis=1, keepdims=True)

        def scaled(factor):
            q = grad[k] * factor
            grad[k] = q
            q = q * UP
            mv_own[k, 1:2] = jnp.sum(q * q, axis=0, keepdims=True)

        @pl.when(k < WIDE)
        def _():
            scaled(column(k))

        @pl.when(k >= WIDE)
        def _():
            factor = column(4 * k - 15)
            for q in (2, 1, 0):
                factor = jnp.where(col < THIN * q + THIN, column(4 * k - 18 + q), factor)
            scaled(factor)
        core_copy(k).start()

    def stage_y(k):
        core_copy(k).wait_recv()
        mv_one[k] = mv_own[k] + mv_core[k]
        start(y_copies(k))

    def stage_z(k):
        mv_two[k] = collect(mv_one.at[k], mv_y.at[k], y_copies(k))
        start(z_copies(k))

    def model_side(k):
        mine = mats_of(k)
        v = collect(mv_two.at[k], mv_z.at[k], z_copies(k))
        new = BETA_TWO * mv_mom[k] + (1.0 - BETA_TWO) * (v[0:1] / D)
        mv_new[k] = new
        inv = 1.0 / jnp.sqrt(new)
        a = jnp.sqrt(v[1:2]) * inv * (1.0 / UP)
        a = a * a
        u = grad[k] * inv
        rows = jnp.where(mine, v[2:3, 0:LANES] / 4, sc_own[1:2])

        @pl.when(k < WIDE)
        def _():
            sc_own[0:1] = jnp.where(mine, total(a), sc_own[0:1])
            sc_own[1:2] = jnp.where(jnp.logical_and(mine, lane >= 4), total(new), rows)
            grad[k] = u

        @pl.when(k >= WIDE)
        def _():
            upd, row = sc_own[0:1], rows
            for q in range(4):
                j = 4 * k - 18 + q
                upd = jnp.where(lane == j, total(jnp.where(of_mat(q), a, 0.0)), upd)
                row = jnp.where(jnp.logical_and(lane == j, lane >= 15), total(jnp.where(of_mat(q), new, 0.0)), row)
                if q % 2 == 0:
                    gsm[j - WIDE] = u[:, THIN * q:THIN * q + THIN]
                else:
                    gsm[j - WIDE] = pltpu.roll(u[:, THIN * q - 64:THIN * q + THIN], THIN, 1)[:, :THIN]
            sc_own[0:1] = upd
            sc_own[1:2] = row
            sc_own[2:3] = v[2:3, LANES:PAIR]

    stages = ((0, stage_split), (LAG_ADD, stage_add), (LAG_RELAY1, lambda s: relay(True, s)), (LAG_TURN, stage_turn),
              (LAG_RELAY2, lambda s: relay(False, s)), (LAG_SUM, stage_sum))
    slab_stages = ((LAG_SUM, sums), (LAG_DV, data_side), (LAG_CORE, stage_y), (LAG_Y, stage_z), (LAG_Z, model_side))

    def trip(i, carry):
        for lag, stage in stages:
            @pl.when(jnp.logical_and(i >= lag, i < STEPS + lag))
            def _(lag=lag, stage=stage):
                stage(i - lag)

        @pl.when(i == LAG_RELAY1)
        def _():
            prepare()
        for lag, stage in slab_stages:
            e = i - lag - (CUTS - 1)

            @pl.when(jnp.logical_and(jnp.logical_and(e >= 0, e < STEPS), lax.rem(e + STEPS, CUTS) == 0))
            def _(e=e, stage=stage):
                stage(e // CUTS)
        return carry
    lax.fori_loop(0, STEPS + LAG_Z, trip, 0)

    sc_cp = spread('x', sc_own, sc_got, sc_s, sc_r)
    start(sc_cp)

    square[0:BLK] = dv_all[...]
    turned = square[...].T
    r_in_n[...] = turned[0:4, 0:BLK]
    c_out_n[...] = turned[4:6, 0:BLK]
    r_qkv_n[...] = turned[6:15, 0:BLK]
    c_o_n[...] = turned[15:18, 0:BLK]
    for k in range(4):
        c_in_n[k:k + 1] = mv_new[k]
    for k in range(2):
        r_out_n[k:k + 1] = mv_new[4 + k]
    for j in range(12):
        k, q = WIDE + j // 4, j % 4
        if q % 2 == 0:
            thin_a[j:j + 1, 0:THIN] = mv_new[k, :, THIN * q:THIN * q + THIN]
        else:
            thin_b[j:j + 1] = mv_new[k, :, THIN * q - 64:THIN * q + THIN]
    odd = lax.rem(lax.broadcasted_iota(jnp.int32, thin_a.shape, 0), 2) == 1
    thin_a[...] = jnp.where(odd, pltpu.roll(thin_b[...], THIN, 1), thin_a[...])
    c_qkv_n[...] = thin_a[0:9, 0:THIN]
    r_o_n[...] = thin_a[9:12, 0:THIN]

    def drain(s, carry):
        for h in range(2):
            d2d(s, h).wait_send()
            for buf, sem in ((s0.at[s, h, pl.ds(0, 3)], p1_s), (b2.at[s, h, pl.ds(0, 3)], p2_s)):
                local(buf, buf, sem.at[s, h]).wait()
        return carry
    lax.fori_loop(0, STEPS, drain, 0)

    def drain_slab(k, carry):
        for cp in dv_copies(k) + [core_copy(k)] + y_copies(k) + z_copies(k):
            cp.wait_send()
        return carry
    lax.fori_loop(0, SLABS, drain_slab, 0)

    sc = collect(sc_own, sc_got, sc_cp)
    full = jnp.where(lane < WIDE, FF * D, D * D)
    rows = jnp.where(jnp.logical_and(lane >= 4, lane < 6), FF, D)
    row_mean = sc[1:2] / rows
    upd_rms = jnp.sqrt(row_mean * (sc[0:1] / full))
    w_rms = jnp.sqrt(sc[2:3] / full)
    scale = LR_BASE * jnp.maximum(1e-3, w_rms) * (jnp.sqrt(row_mean) / jnp.maximum(1.0, upd_rms))
    for j in range(MATS):
        upd = grad[j] if j < WIDE else gsm[j - WIDE]
        new = weight_of(j) - scale[:, j:j + 1] * upd
        if j < 4:
            w_in_n[j] = new
        elif j < 6:
            w_out_n[j - 4] = new
        elif j < 15:
            w_qkv_n[j - 6] = new
        else:
            w_o_n[j - 15] = new
    for cp in sc_cp:
        cp.wait_send()


def write_out(*refs):
    n = len(refs) // 2
    copies = [pltpu.make_async_copy(refs[j], refs[n + j], refs[-1].at[j]) for j in range(n)]
    for cp in copies:
        cp.start()
    for cp in copies:
        cp.wait()


def solution(mesh):
    rows_data = (P('data', None, None, 'model'), P(None, 'data', 'model'), P(None, 'data'), P(None, 'model'))
    rows_model = (P('data', None, 'model', None), P(None, 'model', 'data'), P(None, 'model'), P(None, 'data'))
    DMA = pltpu.SemaphoreType.DMA

    def step_all(grad_in, w_in, row_in, col_in, grad_out, w_out, row_out, col_out,
                 grad_qkv, w_qkv, row_qkv, col_qkv, grad_o, w_o, row_o, col_o):
        args = (grad_in[0], w_in, row_in, col_in,
                grad_out[0], w_out.swapaxes(1, 2), row_out, col_out,
                grad_qkv[0].swapaxes(1, 2).reshape(-1, DIM), w_qkv, row_qkv, col_qkv,
                grad_o[0].reshape(-1, DIM), w_o.swapaxes(1, 2), row_o, col_o)
        small = [a for n, a in enumerate(args) if n % 4]
        outs = [jax.ShapeDtypeStruct(a.shape, a.dtype) for a in small]
        held = [pltpu.VMEM(a.shape, a.dtype) for a in small]
        vm = lambda *s: pltpu.VMEM(s, F32)
        res = pl.pallas_call(
            kernel,
            out_shape=held,
            in_specs=[pl.BlockSpec(memory_space=pl.ANY)] * len(args),
            out_specs=[pl.BlockSpec(memory_space=pltpu.VMEM)] * len(outs),
            scratch_shapes=[
                pltpu.VMEM((SLABS, DIM, DIM), jnp.bfloat16),
                vm(STEPS, 2, 4, 4, BLK, CW), vm(STEPS, 2, 4, 4, BLK, CW),
                vm(STEPS, 2, 2, 2, BLK, CW), vm(STEPS, 2, 2, 4, BLK, CW), vm(STEPS, 2, 4, BLK, CW),
                vm(STEPS, 2, 2, 16, CW), vm(STEPS, 2, 2, BLK, CW),
                vm(SLABS, BLK, DIM), vm(12, BLK, THIN),
                vm(THIN, HALF), pltpu.VMEM((2, THIN, HALF), jnp.bfloat16)]
            + [vm(*a.shape) for n, a in enumerate(small) if n % 3 == 0] + [vm(*a.shape) for n, a in enumerate(small) if n % 3]
            + [vm(LANES, LANES), vm(16, PAIR), vm(16, PAIR), vm(BLK, LANES), vm(BLK, LANES),
               vm(SLABS, BLK, LANES), vm(SLABS, 4, BLK, LANES), vm(SLABS, 1, DIM), vm(SLABS, 1, DIM),
               vm(SLABS, 4, DIM), vm(SLABS, 4, DIM), vm(SLABS, 4, DIM), vm(SLABS, 4, 4, DIM), vm(SLABS, 4, DIM),
               vm(SLABS, 4, 4, DIM), vm(8, LANES), vm(4, 8, LANES),
               DMA((SLABS + 1,)), DMA((len(small),)), DMA((STEPS, 2)), DMA((STEPS, 2)),
               DMA((STEPS, 2)), DMA((STEPS, 2, 3)), DMA((STEPS, 2)), DMA((STEPS, 2, 3)),
               DMA((SLABS, 4)), DMA((SLABS, 4)), DMA((3, SLABS, 4)), DMA((3, SLABS, 4)), DMA((4,)), DMA((4,))],
            compiler_params=pltpu.CompilerParams(
                collective_id=0, has_side_effects=True, vmem_limit_bytes=58_000_000),
            name='adafactor',
        )(*args)
        res = list(pl.pallas_call(
            write_out,
            out_shape=outs,
            in_specs=[pl.BlockSpec(memory_space=pltpu.VMEM)] * len(outs),
            out_specs=[pl.BlockSpec(memory_space=pl.ANY)] * len(outs),
            scratch_shapes=[DMA((len(outs),))],
            name='write_out',
        )(*[pltpu.with_memory_space_constraint(r, pltpu.VMEM) for r in res]))
        for n in (3, SLABS):
            res[n] = res[n].swapaxes(1, 2)
        return tuple(res)

    in_specs = rows_data + rows_model + rows_data + rows_model
    out_specs = rows_data[1:] + rows_model[1:] + rows_data[1:] + rows_model[1:]
    return jax.shard_map(step_all, mesh=mesh, in_specs=in_specs, out_specs=out_specs, check_vma=False)
```

time: 603 us -> 94.4 us (0.16)
  waiting for transfers between devices: 336 us -> 0 us
  blocking collectives: 210 us -> 0 us
  Pallas kernels: 0 us -> 93.6 us
  other arithmetic: 31.4 us -> 0 us
  between operations: 14.1 us -> 0.66 us
  local copies, waits for them, and re-layouts: 9.49 us -> 0 us
    reduce_scatter x4 -> x0, waiting for transfers between devices: 336 us -> none  [update_block(): lax.psum_scatter(grad_parts[0].astype(jnp.float32), 'data', scatter_dimen...]
    psum x4 -> x0, blocking collectives: 210 us -> none  [the longest x2 132 us: update_block(): col_sum = lax.psum(jnp.sum(grad_sq, axis=1), row_axis)]
    pallas_call x0 -> x2, Pallas kernels: none -> 93.6 us  [the longest x1 92.6 us: step_all(): pl.pallas_call(kernel, out_shape=held, in_specs=[pl.BlockSpec(memory_spac...]
    convert_element_type x4 -> x0, other arithmetic: 14.4 us -> none  [update_block(): grad_parts[0].astype(jnp.float32)]
    reduce_sum x16 -> x0, other arithmetic: 9.67 us -> none  [the longest x4 4.53 us: finish_update(): jnp.sum(update * update, axis=(1, 2), keepdims=True)]
    unnamed x43 -> x0, local copies, waits for them, and re-layouts: 9.49 us -> none
    sub x4 -> x0, other arithmetic: 6.91 us -> none  [finish_update(): weight - LR_BASE * jnp.maximum(0.001, w_rms) * update]
  transfers between devices with their start and end apart: 4 -> 0, of which waited for: 4 -> 0; matrix products, arithmetic and copies ran while one was open for 4% -> 0% of each run, Pallas kernels for 0% -> 0%
where the time goes in v2:
time: 94.4 us; the launch traced here: 94.3 us
  Pallas kernels  93.6 us (99%)
    pallas_call x1, Pallas kernels, step_all(): pl.pallas_call(kernel, out_shape=held, in_specs=[pl.BlockSpec(memory_spac...  92.6 us

profile of v2, /device:TPU:0, one launch (start us, length us, event | category | flops | bytes accessed | tf_op | source)
XLA Modules:
  0.0 94.3 jit_solution(12706165255475735341)
XLA Ops:
  0.7 92.6 %adafactor.1 = (f32[4,24,768]{2,1,0:T(8,128)S(1)}, f32[4,24]{1,0:T(4,128)S(1)}, f32[4,768]{1,0:T(4,128)S(1)}, f32[2,24,768]{2,1,0:T(8,128)S(1)}, f32[2,768]{1,0:...) custom-call(bf16[4,768,768]{2,1,0:T(8,128)(2,1)} %bitcast.12, ...), custom_call_target="tpu_custom_call" | custom-call | tf_op jit(solution)/shard_map/adafactor/pallas_call | solution.py:475
  93.3 1.0 %write_out.1 = (f32[4,24,768]{2,1,0:T(8,128)}, f32[4,24]{1,0:T(4,128)}, f32[4,768]{1,0:T(4,128)}, f32[2,24,768]{2,1,0:T(8,128)}, f32[2,768]{1,0:T(2,128)}, /*ind...) custom-call(f32[4,24,768]{2,1,0:T(8,128)S(1)} %get-tuple-element.36., ...), custom_call_target="tpu_custom_call" | custom-call | tf_op jit(solution)/shard_map/write_out/pallas_call | solution.py:499

commit v3 on v2

v3 whole, which is shorter than its diff:
```python
import jax
import jax.numpy as jnp
from jax import lax
from jax.experimental import pallas as pl
from jax.experimental.pallas import tpu as pltpu
from jax.sharding import PartitionSpec as P

OPT_STEP = 4
EPS_SQ = 1e-30
BETA_TWO = 1.0 - OPT_STEP ** -0.8
LR_BASE = min(1e-2, OPT_STEP ** -0.5)

F32 = jnp.float32
MESH = pl.DeviceIdType.MESH
FF, D = 3072.0, 768.0
DIM = 768
THIN = 192
LANES = 128
PAIR = 256
SLABS = 9
PLAIN = 4
WIDE = 6
MATS = 18
STEPS = SLABS
HALF = 384
BLK = 24
ROWCUT = (16, 8)
UP = 2.0 ** 48

HELD = 1
LAG_ADD, LAG_RELAY, LAG_TURN, LAG_RELAY2, LAG_SUM, LAG_DATA, LAG_Z, LAG_MODEL = range(1, 9)


OTHERS = (1, 2, 3)
HALVES = range(2)
THREE = pl.ds(1, 3)
FIRST, SECOND, THIRD = (slice(n, n + 1) for n in range(3))
IN, OUT, QKV, O = slice(4), slice(4, 6), slice(6, 15), slice(15, 18)


def down(v):
    return jnp.sum(v, axis=0, keepdims=True)


def along(v):
    return jnp.sum(v, axis=1, keepdims=True)


def mod4(v):
    return lax.rem(v + 8, 4)


def cut(h, piece):
    return pl.ds(0, ROWCUT[h]) if piece == 0 else pl.ds(ROWCUT[h], BLK - ROWCUT[h])


def slab_of(s):
    if isinstance(s, int):
        return (0, 1, 6, 7, 8, 4, 5, 2, 3)[s]
    return jnp.where(s < 2, s, jnp.where(s < 5, s + 4, jnp.where(s < 7, s - 1, s - 5)))


def kernel(g_in, w_in, r_in, c_in, g_out, w_out, r_out, c_out, g_qkv, w_qkv, r_qkv, c_qkv, g_o, w_o, r_o, c_o,
           w_in_n, r_in_n, c_in_n, w_out_n, r_out_n, c_out_n, w_qkv_n, r_qkv_n, c_qkv_n, w_o_n, r_o_n, c_o_n,
           xin, s0, r0, r1a, r1b, b2, r2a, r2b, grad, gsm, pick_f, pick, vw_in, vw_out, vw_qkv, vw_o,
           vr_in, vc_in, vr_out, vc_out, vr_qkv, vc_qkv, vr_o, vc_o,
           square, thin_a, thin_b, dv_mom, dv_all, dv_own, dv_got, mv_mom, mv_new, mv_own, mv_y, mv_two, mv_z,
           sc_own, sc_got, ld_sem, sm_sem, sent, d2d_r, p1_r, p2_r, dv_r, y_r, z_r, sc_r):
    d = lax.axis_index('data')
    x = lax.axis_index('model')
    core = lax.rem(d, 2)
    y = lax.rem(d // 2, 4)
    z = d // 8

    def at(axis, off, other=0):
        if axis == 'x':
            return {'model': lax.rem(x + off, 4)}
        if axis == 'y':
            return {'data': (z * 4 + lax.rem(y + off, 4)) * 2 + (1 - core if other else core)}
        if axis == 'z':
            return {'data': (lax.rem(z + off, 4) * 4 + y) * 2 + core}
        return {'data': (z * 4 + y) * 2 + (1 - core)}

    def local(src, dst, sem):
        return pltpu.make_async_copy(src, dst, sem)

    loads = [local(g_in.at[k], xin.at[k], ld_sem.at[k]) for k in range(PLAIN)]
    loads += [local(g_out.at[k - PLAIN], xin.at[k], ld_sem.at[k]) for k in range(PLAIN, WIDE)]
    loads += [local(g_qkv.at[pl.ds(DIM * k, DIM)], xin.at[WIDE + k], ld_sem.at[WIDE + k]) for k in HALVES]
    loads += [local(g_qkv.at[pl.ds(2 * DIM, THIN)], xin.at[SLABS - 1, pl.ds(0, THIN)], ld_sem.at[SLABS - 1]),
              local(g_o, xin.at[SLABS - 1, pl.ds(THIN, DIM - THIN)], ld_sem.at[SLABS])]
    small = [(w_in, vw_in), (w_out, vw_out), (w_qkv, vw_qkv), (w_o, vw_o), (r_in, vr_in), (c_in, vc_in),
             (r_out, vr_out), (c_out, vc_out), (r_qkv, vr_qkv), (c_qkv, vc_qkv), (r_o, vr_o), (c_o, vc_o)]
    small = [local(s, t, sm_sem.at[j]) for j, (s, t) in enumerate(small)]
    for cp in [loads[slab_of(j)] for j in range(SLABS)] + loads[SLABS:] + small:
        cp.start()

    barrier = pltpu.get_barrier_semaphore()
    peers = [at('c', 1)] + [at(a, j) for a in 'yzx' for j in OTHERS] + [at('y', j, 1) for j in OTHERS]
    for p in peers:
        pl.semaphore_signal(barrier, inc=1, device_id=p, device_id_type=MESH)
    pl.semaphore_wait(barrier, len(peers))

    def remote(src, dst, ss, rs, dev):
        return pltpu.make_async_remote_copy(src_ref=src, dst_ref=dst, send_sem=ss, recv_sem=rs,
                                            device_id=dev, device_id_type=MESH)

    def d2d(s, h):
        return remote(s0.at[s, h], r0.at[s, h], sent.at[0], d2d_r.at[s, h], at('c', 1))

    def make_pick():
        for side in HALVES:
            cc = (1 - core) if side == 0 else core
            row = lax.broadcasted_iota(jnp.int32, (BLK, HALF), 0)
            col = lax.broadcasted_iota(jnp.int32, (BLK, HALF), 1)
            for b in range(8):
                pick_f[pl.ds(BLK * b, BLK)] = jnp.where(col == row + 2 * BLK * b + BLK * cc, 1.0, 0.0)
            pick[side] = pick_f[...].astype(jnp.bfloat16)

    def part(s, h, side, fn):
        k = slab_of(s)

        def plain():
            first = (core == 0) if side == 1 else (core == 1)
            for g in range(16):
                v = xin[k, pl.ds(2 * BLK * g, 2 * BLK), pl.ds(HALF * h, HALF)].astype(F32)
                fn(pl.ds(g // 4, 1), pl.ds(g % 4, 1), jnp.where(first, v[:BLK], v[BLK:]).reshape(1, 1, BLK, HALF))

        def turned():
            for g in HALVES:
                v = xin[k, pl.ds(HALF * h, HALF), pl.ds(HALF * g, HALF)]
                v = lax.dot_general(pick[side], v, (((1,), (1,)), ((), ())), preferred_element_type=F32)
                fn(pl.ds(2 * g, 2), slice(None), v.reshape(2, 4, BLK, HALF))
        choose(k < PLAIN, plain, turned)

    def choose(cond, yes, no):
        if isinstance(cond, bool):
            return yes() if cond else no()
        pl.when(cond)(yes)
        pl.when(jnp.logical_not(cond))(no)

    def stage_split(s):
        for j in range(SLABS):
            @pl.when(slab_of(s) == j)
            def _(j=j):
                loads[j].wait()
                if j == SLABS - 1:
                    loads[SLABS].wait()
        for h in HALVES:
            def put(zs, ys, v, h=h):
                s0[s, h, zs, ys] = v
            part(s, h, 0, put)
            d2d(s, h).start()

    def ring(h, first):
        axis = ('y', 'z')[h] if first else ('z', 'y')[h]
        return axis, (y if axis == 'y' else z)

    def block(first, s, h, t, piece, flip):
        if not first:
            return b2.at[s, h, t, cut(h ^ flip, piece)]
        return r0.at[s, 0, pl.ds(2 * piece, 2), t] if h == 0 else r0.at[s, 1, t, pl.ds(2 * piece, 2)]

    PLAN = ((-2, 0, 0), (2, 1, 1), (-1, 1, 0), (1, 0, 1), (-1, 0, 0), (1, 1, 1))

    def passing(first, s, h, m, flip):
        _, piece, way = PLAN[m]
        return r1a.at[s, h, way] if first else r2a.at[s, h, way, pl.ds(0, cut(h ^ flip, piece).size)]

    def msg(first, s, h, m, flip):
        axis, n = ring(h, first)
        off, piece, way = PLAN[m]
        recv, landed = (p1_r, r1b) if first else (p2_r, r2b)
        src = block(first, s, h, mod4(n + off), piece, flip)
        if m < 2:
            dst = passing(first, s, h, m, flip)
        else:
            dst = landed.at[s, h, way, pl.ds(2 * piece, 2) if first else cut(h ^ flip, piece)]
        return remote(src, dst, sent.at[1 if first else 2], recv.at[s, h if m < 2 else 2], at(axis, 1 if way else 3))

    def send_raw(first, s, h, flip):
        for m in range(4):
            msg(first, s, h, m, flip).start()

    def wait_for(ref, sem):
        local(ref, ref, sem).wait()

    def stage_add(s):
        for h in HALVES:
            d2d(s, h).wait_recv()

            def add(zs, ys, v, h=h):
                r0[s, h, zs, ys] += v
            part(s, h, 1, add)
            send_raw(True, s, h, 0)

    def relay(first, s, flip):
        for h in HALVES:
            n = ring(h, first)[1]
            wait_for(r1a.at[s, h] if first else b2.at[s, h, 0], (p1_r if first else p2_r).at[s, h])
            for m in HALVES:
                off, piece, _ = PLAN[4 + m]
                ref = block(first, s, h, mod4(n + off), piece, flip)
                ref[...] += passing(first, s, h, m, flip)[...]
                msg(first, s, h, 4 + m, flip).start()

    def stage_turn(s, flip):
        wait_for(r1b.at[s], p1_r.at[s, 2])
        for h in HALVES:
            n = ring(h, True)[1]
            own = r0[s, 0, :, n] if h == 0 else r0[s, 1, n]
            b2[s, h] = own + r1b[s, h, 0] + r1b[s, h, 1]
            send_raw(False, s, h, flip)

    def stage_sum(s):
        wait_for(r2b.at[s], p2_r.at[s, 2])
        for h in HALVES:
            n = ring(h, False)[1]
            grad[slab_of(s), :, pl.ds(HALF * h, HALF)] = (b2[s, h, n] + r2b[s, h, 0] + r2b[s, h, 1]) / 32

    lane = lax.broadcasted_iota(jnp.int32, (1, LANES), 1)
    col = lax.broadcasted_iota(jnp.int32, (1, DIM), 1)
    count = jnp.where(lane < WIDE, FF, D)

    def of_mat(q):
        return jnp.logical_and(col >= THIN * q, col < THIN * q + THIN)

    def total(v):
        return along(down(v))

    def place(j):
        n = 0 if j < 4 else 1 if j < 6 else 2 if j < 15 else 3
        return n, j - (0, 4, 6, 15)[n]

    def weight_of(j):
        n, i = place(j)
        return (vw_in, vw_out, vw_qkv, vw_o)[n][i]

    def prepare():
        for cp in small:
            cp.wait()
        square[...] = jnp.zeros_like(square)
        square[IN, :BLK] = vr_in[...]
        square[OUT, :BLK] = vc_out[...]
        square[QKV, :BLK] = vr_qkv[...]
        square[O, :BLK] = vc_o[...]
        dv_mom[...] = square[...].T[:BLK]
        thin_a[...] = jnp.zeros_like(thin_a)
        thin_a[:9, :THIN] = vc_qkv[...]
        thin_a[9:12, :THIN] = vr_o[...]
        thin_b[...] = pltpu.roll(thin_a[...], 64, 1)
        for k in range(4):
            mv_mom[k] = vc_in[k:k + 1]
        for k in HALVES:
            mv_mom[4 + k] = vr_out[k:k + 1]
        for j in range(12):
            k, q = WIDE + j // 4, j % 4
            if q % 2 == 0:
                mv_mom[k, :, THIN * q:THIN * q + THIN] = thin_a[j:j + 1, :THIN]
            else:
                span = slice(THIN * q - 64, THIN * q + THIN)
                mv_mom[k, :, span] = jnp.where(col[:, :PAIR] < 64, mv_mom[k, :, span], thin_b[j:j + 1])
        mv_own[...] = jnp.zeros_like(mv_own)
        sc_own[...] = jnp.zeros_like(sc_own)
        dv_all[...] = jnp.ones_like(dv_all)
        vec = jnp.zeros((1, LANES), F32)
        for j in range(MATS):
            w = weight_of(j)
            vec = jnp.where(lane == j, total(w * w), vec)
        mv_own[slab_of(SLABS - 1), THIRD, LANES:PAIR] = vec

    def spread(axis, src, dst, ss, rs):
        return [remote(src, dst.at[j], ss, rs, at(axis, j)) for j in OTHERS]

    def start(copies):
        for cp in copies:
            cp.start()

    def rows_of(k):
        return pl.ds(0, 3 if isinstance(k, int) and k == slab_of(SLABS - 1) else 2)

    def dv_copies(k):
        return spread('x', dv_own.at[k], dv_got.at[k], sent.at[3], dv_r.at[k])

    def y_copies(k):
        src = mv_own.at[k, rows_of(k)]
        return [remote(src, mv_y.at[k, j + 4 * other, rows_of(k)], sent.at[4 + rows_of(k).size], y_r.at[k],
                       at('y', j, other) if j else at('c', 1)) for j in range(4) for other in HALVES if j or other]

    def z_copies(k):
        return [remote(mv_two.at[k, rows_of(k)], mv_z.at[k, j, rows_of(k)], sent.at[6 + rows_of(k).size], z_r.at[k], at('z', j))
                for j in OTHERS]

    def sums(k):
        g = grad[k]
        s = g * g + EPS_SQ
        mv_own[k, FIRST] = down(s)

        def wide():
            dv_own[k] = jnp.where(lane == k, along(s), 0.0)

        def thin():
            dv = jnp.zeros((BLK, LANES), F32)
            for q in range(4):
                dv = jnp.where(lane == 4 * k - 18 + q, along(jnp.where(of_mat(q), s, 0.0)), dv)
            dv_own[k] = dv
        choose(k < WIDE, wide, thin)
        start(dv_copies(k))

    def mats_of(k):
        low = jnp.where(k < WIDE, k, 4 * k - 18)
        return jnp.logical_and(lane >= low, lane < jnp.where(k < WIDE, k + 1, 4 * k - 14))

    def data_side(k):
        mine = mats_of(k)
        wait_for(dv_got.at[k, THREE], dv_r.at[k])
        got = (dv_own[k] + dv_got[k, 2]) + (dv_got[k, 1] + dv_got[k, 3])
        new = BETA_TWO * dv_mom[...] + (1.0 - BETA_TWO) * (got / count)
        dv_all[...] = jnp.where(mine, new, dv_all[...])
        if rows_of(k).size == 3:
            mv_own[k, THIRD, :LANES] = down(dv_all[...])
        inv = 1.0 / jnp.sqrt(jnp.where(mine, new, 1.0))

        def column(j):
            return along(jnp.where(lane == j, inv, 0.0))

        def scaled(factor):
            q = grad[k] * factor
            grad[k] = q
            q = q * UP
            mv_own[k, SECOND] = down(q * q)

        def wide():
            scaled(column(k))

        def thin():
            factor = column(4 * k - 15)
            for q in (2, 1, 0):
                factor = jnp.where(col < THIN * q + THIN, column(4 * k - 18 + q), factor)
            scaled(factor)
        choose(k < WIDE, wide, thin)
        start(y_copies(k))

    def stage_z(k):
        wait_for(mv_y.at[k, pl.ds(1, 7), rows_of(k)], y_r.at[k])
        one = [mv_own[k] + mv_y[k, 4]] + [mv_y[k, j] + mv_y[k, 4 + j] for j in OTHERS]
        mv_two[k] = (one[0] + one[2]) + (one[1] + one[3])
        start(z_copies(k))

    def model_side(k):
        mine = mats_of(k)
        wait_for(mv_z.at[k, THREE, rows_of(k)], z_r.at[k])
        v = (mv_two[k] + mv_z[k, 2]) + (mv_z[k, 1] + mv_z[k, 3])
        new = BETA_TWO * mv_mom[k] + (1.0 - BETA_TWO) * (v[FIRST] / D)
        mv_new[k] = new
        inv = 1.0 / jnp.sqrt(new)
        a = jnp.sqrt(v[SECOND]) * inv * (1.0 / UP)
        a = a * a
        u = grad[k] * inv

        def wide():
            sc_own[FIRST] = jnp.where(mine, total(a), sc_own[FIRST])
            sc_own[SECOND] = jnp.where(mine, total(new), sc_own[SECOND])
            grad[k] = u

        def thin():
            upd, row = sc_own[FIRST], sc_own[SECOND]
            for q in range(4):
                j = 4 * k - 18 + q
                upd = jnp.where(lane == j, total(jnp.where(of_mat(q), a, 0.0)), upd)
                row = jnp.where(lane == j, total(jnp.where(of_mat(q), new, 0.0)), row)
                if q % 2 == 0:
                    gsm[j - WIDE] = u[:, THIN * q:THIN * q + THIN]
                else:
                    gsm[j - WIDE] = pltpu.roll(u[:, THIN * q - 64:THIN * q + THIN], THIN, 1)[:, :THIN]
            sc_own[FIRST] = upd
            sc_own[SECOND] = row
        choose(k < WIDE, wide, thin)
        if rows_of(k).size == 3:
            by_model = jnp.logical_or(jnp.logical_and(lane >= 4, lane < 6), lane >= 15)
            sc_own[SECOND] = jnp.where(by_model, sc_own[SECOND], v[THIRD, :LANES] / 4)
            sc_own[THIRD] = v[THIRD, LANES:PAIR]

    def by_parity(fn):
        def stage(s):
            choose(lax.rem(s, 2) == 0, lambda: fn(s, 0), lambda: fn(s, 1))
        return stage

    def turn(s):
        stage_turn(s, s % 2)

    def relay2(s):
        relay(False, s, s % 2)

    def finish(s):
        stage_sum(s)
        sums(slab_of(s))

    def relay1(s):
        relay(True, s, 0)

    def data(s):
        data_side(slab_of(s))

    def to_z(s):
        stage_z(slab_of(s))

    def model(s):
        model_side(slab_of(s))

    early = ((0, stage_split), (LAG_ADD, stage_add), (LAG_RELAY, relay1))
    late = ((LAG_TURN, by_parity(stage_turn)), (LAG_RELAY2, by_parity(lambda s, flip: relay(False, s, flip))),
            (LAG_SUM, finish), (LAG_DATA, data), (LAG_Z, to_z), (LAG_MODEL, model))

    def trip(i, carry):
        for lag, stage in early:
            @pl.when(i >= lag)
            def _(lag=lag, stage=stage):
                stage(i - lag)

        @pl.when(i == 1)
        def _():
            make_pick()
        for lag, stage in late:
            @pl.when(jnp.logical_and(i >= lag, i < HELD + lag))
            def _(lag=lag, stage=stage):
                stage(i - lag)

        @pl.when(i == LAG_TURN)
        def _():
            prepare()
        return carry
    lax.fori_loop(0, STEPS, trip, 0)

    last = STEPS - 1
    mids = range(HELD, last - 1)
    held = range(HELD, last)

    def rest(i):
        for lag, stage in ((LAG_TURN, turn), (LAG_RELAY2, relay2), (LAG_SUM, finish), (LAG_DATA, data), (LAG_Z, to_z),
                           (LAG_MODEL, model)):
            if 0 <= i - lag < HELD:
                stage(i - lag)

    def each(stage, steps):
        for s in steps:
            stage(s)
    stage_add(last)
    relay1(last - 1)
    relay1(last)
    each(turn, mids)
    rest(STEPS)
    turn(last - 1)
    turn(last)
    each(relay2, mids)
    rest(STEPS + 1)
    relay2(last - 1)
    relay2(last)
    rest(STEPS + 2)
    each(finish, mids)
    finish(last - 1)
    rest(STEPS + 3)
    finish(last)
    rest(STEPS + 4)
    each(data, held)
    data(last)
    each(to_z, held)
    to_z(last)
    each(model, held)
    model(last)

    sc_cp = spread('x', sc_own, sc_got, sent.at[SLABS + 1], sc_r.at[0])
    start(sc_cp)

    square[:BLK] = dv_all[...]
    turned = square[...].T
    r_in_n[...] = turned[IN, :BLK]
    c_out_n[...] = turned[OUT, :BLK]
    r_qkv_n[...] = turned[QKV, :BLK]
    c_o_n[...] = turned[O, :BLK]
    for k in range(4):
        c_in_n[k:k + 1] = mv_new[k]
    for k in HALVES:
        r_out_n[k:k + 1] = mv_new[4 + k]
    for j in range(12):
        k, q = WIDE + j // 4, j % 4
        if q % 2 == 0:
            thin_a[j:j + 1, :THIN] = mv_new[k, :, THIN * q:THIN * q + THIN]
        else:
            thin_b[j:j + 1] = mv_new[k, :, THIN * q - 64:THIN * q + THIN]
    odd = lax.rem(lax.broadcasted_iota(jnp.int32, thin_a.shape, 0), 2) == 1
    thin_a[...] = jnp.where(odd, pltpu.roll(thin_b[...], THIN, 1), thin_a[...])
    c_qkv_n[...] = thin_a[:9, :THIN]
    r_o_n[...] = thin_a[9:12, :THIN]

    few = STEPS - 1
    for j, ref in enumerate((s0, s0.at[:, :, pl.ds(0, 3)], b2.at[:, :, pl.ds(0, 3)], dv_got.at[:, pl.ds(0, 3)])):
        wait_for(ref, sent.at[j])
    wait_for(mv_y.at[pl.ds(0, few), pl.ds(1, 7), pl.ds(0, 2)], sent.at[6])
    wait_for(mv_y.at[0, pl.ds(1, 7), pl.ds(0, 3)], sent.at[7])
    wait_for(mv_z.at[pl.ds(0, few), THREE, pl.ds(0, 2)], sent.at[8])
    wait_for(mv_z.at[0, THREE, pl.ds(0, 3)], sent.at[9])

    wait_for(sc_got.at[THREE], sc_r.at[0])
    sc = (sc_own[...] + sc_got[2]) + (sc_got[1] + sc_got[3])
    full = jnp.where(lane < WIDE, FF * D, D * D)
    rows = jnp.where(jnp.logical_and(lane >= 4, lane < 6), FF, D)
    row_mean = sc[SECOND] / rows
    upd_rms = jnp.sqrt(row_mean * (sc[FIRST] / full))
    w_rms = jnp.sqrt(sc[THIRD] / full)
    scale = LR_BASE * jnp.maximum(1e-3, w_rms) * (jnp.sqrt(row_mean) / jnp.maximum(1.0, upd_rms))
    for j in range(MATS):
        upd = grad[j] if j < WIDE else gsm[j - WIDE]
        new = weight_of(j) - scale[:, j:j + 1] * upd
        n, i = place(j)
        (w_in_n, w_out_n, w_qkv_n, w_o_n)[n][i] = new
    wait_for(sc_got.at[THREE], sent.at[SLABS + 1])


def write_out(*refs):
    n = len(refs) // 2
    copies = [pltpu.make_async_copy(refs[j], refs[n + j], refs[-1].at[j]) for j in range(n)]
    for cp in copies:
        cp.start()
    for cp in copies:
        cp.wait()


def solution(mesh):
    rows_data = (P('data', None, None, 'model'), P(None, 'data', 'model'), P(None, 'data'), P(None, 'model'))
    rows_model = (P('data', None, 'model', None), P(None, 'model', 'data'), P(None, 'model'), P(None, 'data'))
    DMA = pltpu.SemaphoreType.DMA

    def step_all(grad_in, w_in, row_in, col_in, grad_out, w_out, row_out, col_out,
                 grad_qkv, w_qkv, row_qkv, col_qkv, grad_o, w_o, row_o, col_o):
        args = (grad_in[0], w_in, row_in, col_in,
                grad_out[0], w_out.swapaxes(1, 2), row_out, col_out,
                grad_qkv[0].swapaxes(1, 2).reshape(-1, DIM), w_qkv, row_qkv, col_qkv,
                grad_o[0].reshape(-1, DIM), w_o.swapaxes(1, 2), row_o, col_o)
        small = [a for n, a in enumerate(args) if n % 4]
        outs = [jax.ShapeDtypeStruct(a.shape, a.dtype) for a in small]
        held = [pltpu.VMEM(a.shape, a.dtype) for a in small]
        vm = lambda *s: pltpu.VMEM(s, F32)
        res = pl.pallas_call(
            kernel,
            out_shape=held,
            in_specs=[pl.BlockSpec(memory_space=pl.ANY)] * len(args),
            out_specs=[pl.BlockSpec(memory_space=pltpu.VMEM)] * len(outs),
            scratch_shapes=[
                pltpu.VMEM((SLABS, DIM, DIM), jnp.bfloat16),
                vm(STEPS, 2, 4, 4, BLK, HALF), vm(STEPS, 2, 4, 4, BLK, HALF),
                vm(STEPS, 2, 2, 2, BLK, HALF), vm(STEPS, 2, 2, 4, BLK, HALF), vm(STEPS, 2, 4, BLK, HALF),
                vm(STEPS, 2, 2, 16, HALF), vm(STEPS, 2, 2, BLK, HALF),
                vm(SLABS, BLK, DIM), vm(12, BLK, THIN),
                vm(THIN, HALF), pltpu.VMEM((2, THIN, HALF), jnp.bfloat16)]
            + [vm(*a.shape) for n, a in enumerate(small) if n % 3 == 0] + [vm(*a.shape) for n, a in enumerate(small) if n % 3]
            + [vm(LANES, LANES), vm(16, PAIR), vm(16, PAIR), vm(BLK, LANES), vm(BLK, LANES),
               vm(SLABS, BLK, LANES), vm(SLABS, 4, BLK, LANES), vm(SLABS, 1, DIM), vm(SLABS, 1, DIM),
               vm(SLABS, 4, DIM), vm(SLABS, 8, 4, DIM), vm(SLABS, 4, DIM), vm(SLABS, 4, 4, DIM), vm(8, LANES), vm(4, 8, LANES),
               DMA((SLABS + 1,)), DMA((len(small),)), DMA((SLABS + 2,)), DMA((STEPS, 2)), DMA((STEPS, 3)), DMA((STEPS, 3)),
               DMA((SLABS,)), DMA((SLABS,)), DMA((SLABS,)), DMA((1,))],
            compiler_params=pltpu.CompilerParams(
                collective_id=0, has_side_effects=True, vmem_limit_bytes=58_000_000),
            name='adafactor',
        )(*args)
        res = list(pl.pallas_call(
            write_out,
            out_shape=outs,
            in_specs=[pl.BlockSpec(memory_space=pltpu.VMEM)] * len(outs),
            out_specs=[pl.BlockSpec(memory_space=pl.ANY)] * len(outs),
            scratch_shapes=[DMA((len(outs),))],
            name='write_out',
        )(*[pltpu.with_memory_space_constraint(r, pltpu.VMEM) for r in res]))
        for n in (3, SLABS):
            res[n] = res[n].swapaxes(1, 2)
        return tuple(res)

    in_specs = rows_data + rows_model + rows_data + rows_model
    out_specs = rows_data[1:] + rows_model[1:] + rows_data[1:] + rows_model[1:]
    return jax.shard_map(step_all, mesh=mesh, in_specs=in_specs, out_specs=out_specs, check_vma=False)
```

time: 94.4 us -> 84.2 us (0.89)
  Pallas kernels: 93.6 us -> 83.4 us
    pallas_call x1, Pallas kernels: 92.6 us -> 82.4 us  [step_all(): pl.pallas_call(kernel, out_shape=held, in_specs=[pl.BlockSpec(memory_spac...]
where the time goes in v3:
time: 84.2 us; the launch traced here: 84.1 us
  Pallas kernels  83.4 us (99%)
    pallas_call x1, Pallas kernels, step_all(): pl.pallas_call(kernel, out_shape=held, in_specs=[pl.BlockSpec(memory_spac...  82.4 us

profile of v3, /device:TPU:0, one launch (start us, length us, event | category | flops | bytes accessed | tf_op | source)
XLA Modules:
  0.0 84.1 jit_solution(16519243655542109975)
XLA Ops:
  0.7 82.4 %adafactor.1 = (f32[4,24,768]{2,1,0:T(8,128)S(1)}, f32[4,24]{1,0:T(4,128)S(1)}, f32[4,768]{1,0:T(4,128)S(1)}, f32[2,24,768]{2,1,0:T(8,128)S(1)}, f32[2,768]{1,0:...) custom-call(bf16[4,768,768]{2,1,0:T(8,128)(2,1)} %bitcast.12, ...), custom_call_target="tpu_custom_call" | custom-call | tf_op jit(solution)/shard_map/adafactor/pallas_call | solution.py:544
  83.1 1.0 %write_out.1 = (f32[4,24,768]{2,1,0:T(8,128)}, f32[4,24]{1,0:T(4,128)}, f32[4,768]{1,0:T(4,128)}, f32[2,24,768]{2,1,0:T(8,128)}, f32[2,768]{1,0:T(2,128)}, /*ind...) custom-call(f32[4,24,768]{2,1,0:T(8,128)S(1)} %get-tuple-element.36., ...), custom_call_target="tpu_custom_call" | custom-call | tf_op jit(solution)/shard_map/write_out/pallas_call | solution.py:566

commit v4 on v3

--- a/solution.py
+++ b/solution.py
@@ -27,14 +27,15 @@
 ROWCUT = (16, 8)
 UP = 2.0 ** 48
 
-HELD = 1
-LAG_ADD, LAG_RELAY, LAG_TURN, LAG_RELAY2, LAG_SUM, LAG_DATA, LAG_Z, LAG_MODEL = range(1, 9)
+GROUPS = tuple(range(n, min(n + 2, STEPS)) for n in range(0, STEPS, 2))
+PARTS = 3
 
 
 OTHERS = (1, 2, 3)
 HALVES = range(2)
-THREE = pl.ds(1, 3)
-FIRST, SECOND, THIRD = (slice(n, n + 1) for n in range(3))
+THREE, SEVEN = pl.ds(1, 3), pl.ds(1, 7)
+DUO, TRIO = pl.ds(0, 2), pl.ds(0, 3)
+FIRST, SECOND, THIRD, FOURTH = (slice(n, n + 1) for n in range(4))
 IN, OUT, QKV, O = slice(4), slice(4, 6), slice(6, 15), slice(15, 18)
 
 
@@ -48,6 +49,10 @@
 
 def mod4(v):
     return lax.rem(v + 8, 4)
+
+
+def span(h, c):
+    return pl.ds(HALF * h + LANES * c, LANES)
 
 
 def cut(h, piece):
@@ -65,7 +70,7 @@
            xin, s0, r0, r1a, r1b, b2, r2a, r2b, grad, gsm, pick_f, pick, vw_in, vw_out, vw_qkv, vw_o,
            vr_in, vc_in, vr_out, vc_out, vr_qkv, vc_qkv, vr_o, vc_o,
            square, thin_a, thin_b, dv_mom, dv_all, dv_own, dv_got, mv_mom, mv_new, mv_own, mv_y, mv_two, mv_z,
-           sc_own, sc_got, ld_sem, sm_sem, sent, d2d_r, p1_r, p2_r, dv_r, y_r, z_r, sc_r):
+           sc_own, sc_got, ld_sem, sm_sem, sent, first_r, d2d_r, passed, whole, dv_r, sc_r):
     d = lax.axis_index('data')
     x = lax.axis_index('model')
     core = lax.rem(d, 2)
@@ -84,7 +89,7 @@
     def local(src, dst, sem):
         return pltpu.make_async_copy(src, dst, sem)
 
-    loads = [local(g_in.at[k], xin.at[k], ld_sem.at[k]) for k in range(PLAIN)]
+    loads = [None] + [local(g_in.at[k], xin.at[k], ld_sem.at[k]) for k in range(1, PLAIN)]
     loads += [local(g_out.at[k - PLAIN], xin.at[k], ld_sem.at[k]) for k in range(PLAIN, WIDE)]
     loads += [local(g_qkv.at[pl.ds(DIM * k, DIM)], xin.at[WIDE + k], ld_sem.at[WIDE + k]) for k in HALVES]
     loads += [local(g_qkv.at[pl.ds(2 * DIM, THIN)], xin.at[SLABS - 1, pl.ds(0, THIN)], ld_sem.at[SLABS - 1]),
@@ -92,21 +97,22 @@
     small = [(w_in, vw_in), (w_out, vw_out), (w_qkv, vw_qkv), (w_o, vw_o), (r_in, vr_in), (c_in, vc_in),
              (r_out, vr_out), (c_out, vc_out), (r_qkv, vr_qkv), (c_qkv, vc_qkv), (r_o, vr_o), (c_o, vc_o)]
     small = [local(s, t, sm_sem.at[j]) for j, (s, t) in enumerate(small)]
-    for cp in [loads[slab_of(j)] for j in range(SLABS)] + loads[SLABS:] + small:
+    loads[0] = [local(g_in.at[0, :, span(h, c)], xin.at[0, :, span(h, c)], ld_sem.at[SLABS + 1 + h + 2 * c])
+                for c in range(PARTS) for h in HALVES]
+    for cp in loads[0] + [loads[1]]:
         cp.start()
 
     barrier = pltpu.get_barrier_semaphore()
     peers = [at('c', 1)] + [at(a, j) for a in 'yzx' for j in OTHERS] + [at('y', j, 1) for j in OTHERS]
     for p in peers:
         pl.semaphore_signal(barrier, inc=1, device_id=p, device_id_type=MESH)
-    pl.semaphore_wait(barrier, len(peers))
 
     def remote(src, dst, ss, rs, dev):
         return pltpu.make_async_remote_copy(src_ref=src, dst_ref=dst, send_sem=ss, recv_sem=rs,
                                             device_id=dev, device_id_type=MESH)
 
     def d2d(s, h):
-        return remote(s0.at[s, h], r0.at[s, h], sent.at[0], d2d_r.at[s, h], at('c', 1))
+        return remote(s0.at[s, h], r0.at[s, h], sent.at[0], d2d_r.at[s], at('c', 1))
 
     def make_pick():
         for side in HALVES:
@@ -117,14 +123,14 @@
                 pick_f[pl.ds(BLK * b, BLK)] = jnp.where(col == row + 2 * BLK * b + BLK * cc, 1.0, 0.0)
             pick[side] = pick_f[...].astype(jnp.bfloat16)
 
-    def part(s, h, side, fn):
+    def part(s, h, side, fn, cols=None):
         k = slab_of(s)
 
         def plain():
             first = (core == 0) if side == 1 else (core == 1)
             for g in range(16):
-                v = xin[k, pl.ds(2 * BLK * g, 2 * BLK), pl.ds(HALF * h, HALF)].astype(F32)
-                fn(pl.ds(g // 4, 1), pl.ds(g % 4, 1), jnp.where(first, v[:BLK], v[BLK:]).reshape(1, 1, BLK, HALF))
+                v = xin[k, pl.ds(2 * BLK * g, 2 * BLK), cols or pl.ds(HALF * h, HALF)].astype(F32)
+                fn(pl.ds(g // 4, 1), pl.ds(g % 4, 1), jnp.where(first, v[:BLK], v[BLK:]).reshape(1, 1, BLK, -1))
 
         def turned():
             for g in HALVES:
@@ -140,17 +146,24 @@
         pl.when(jnp.logical_not(cond))(no)
 
     def stage_split(s):
-        for j in range(SLABS):
+        for j in range(1, SLABS):
             @pl.when(slab_of(s) == j)
             def _(j=j):
                 loads[j].wait()
                 if j == SLABS - 1:
                     loads[SLABS].wait()
         for h in HALVES:
-            def put(zs, ys, v, h=h):
-                s0[s, h, zs, ys] = v
-            part(s, h, 0, put)
+            split_half(s, h)
             d2d(s, h).start()
+
+    def split_half(s, h):
+        def put(zs, ys, v):
+            s0[s, h, zs, ys] = v
+        part(s, h, 0, put)
+
+    def first_d2d(h, c):
+        cols = span(0, c)
+        return remote(s0.at[0, h, :, :, :, cols], r0.at[0, h, :, :, :, cols], sent.at[0], first_r.at[h, c], at('c', 1))
 
     def ring(h, first):
         axis = ('y', 'z')[h] if first else ('z', 'y')[h]
@@ -167,37 +180,59 @@
         _, piece, way = PLAN[m]
         return r1a.at[s, h, way] if first else r2a.at[s, h, way, pl.ds(0, cut(h ^ flip, piece).size)]
 
-    def msg(first, s, h, m, flip):
+    def msg(first, s, h, m, flip, cols=slice(None)):
         axis, n = ring(h, first)
         off, piece, way = PLAN[m]
-        recv, landed = (p1_r, r1b) if first else (p2_r, r2b)
+        landed = r1b if first else r2b
         src = block(first, s, h, mod4(n + off), piece, flip)
         if m < 2:
             dst = passing(first, s, h, m, flip)
         else:
             dst = landed.at[s, h, way, pl.ds(2 * piece, 2) if first else cut(h ^ flip, piece)]
-        return remote(src, dst, sent.at[1 if first else 2], recv.at[s, h if m < 2 else 2], at(axis, 1 if way else 3))
-
-    def send_raw(first, s, h, flip):
+        if first:
+            src, dst = src.at[:, :, cols], dst.at[:, :, cols]
+        return remote(src, dst, sent.at[1 if first else 2], passed.at[s] if m < 2 else whole.at[s] if first else d2d_r.at[s], at(axis, 1 if way else 3))
+
+    def send_raw(first, s, h, flip, cols=slice(None)):
         for m in range(4):
-            msg(first, s, h, m, flip).start()
+            msg(first, s, h, m, flip, cols).start()
 
     def wait_for(ref, sem):
         local(ref, ref, sem).wait()
 
     def stage_add(s):
+        wait_for(r0.at[s], d2d_r.at[s])
         for h in HALVES:
-            d2d(s, h).wait_recv()
 
             def add(zs, ys, v, h=h):
                 r0[s, h, zs, ys] += v
             part(s, h, 1, add)
             send_raw(True, s, h, 0)
 
+    def first_split():
+        for c in range(PARTS):
+            for h in HALVES:
+                def put(zs, ys, v, h=h, c=c):
+                    s0[0, h, zs, ys, :, span(0, c)] = v
+                loads[0][h + 2 * c].wait()
+                part(0, h, 0, put, span(h, c))
+                if h == 0 and c == 0:
+                    pl.semaphore_wait(barrier, len(peers))
+                first_d2d(h, c).start()
+
+    def first_add():
+        for c in range(PARTS):
+            for h in HALVES:
+                def add(zs, ys, v, h=h, c=c):
+                    r0[0, h, zs, ys, :, span(0, c)] += v
+                first_d2d(h, c).wait_recv()
+                part(0, h, 1, add, span(h, c))
+                send_raw(True, 0, h, 0, span(0, c))
+
     def relay(first, s, flip):
+        wait_for(r1a.at[s] if first else b2.at[s, 0, DUO], passed.at[s])
         for h in HALVES:
             n = ring(h, first)[1]
-            wait_for(r1a.at[s, h] if first else b2.at[s, h, 0], (p1_r if first else p2_r).at[s, h])
             for m in HALVES:
                 off, piece, _ = PLAN[4 + m]
                 ref = block(first, s, h, mod4(n + off), piece, flip)
@@ -205,7 +240,7 @@
                 msg(first, s, h, 4 + m, flip).start()
 
     def stage_turn(s, flip):
-        wait_for(r1b.at[s], p1_r.at[s, 2])
+        wait_for(r1b.at[s], whole.at[s])
         for h in HALVES:
             n = ring(h, True)[1]
             own = r0[s, 0, :, n] if h == 0 else r0[s, 1, n]
@@ -213,7 +248,7 @@
             send_raw(False, s, h, flip)
 
     def stage_sum(s):
-        wait_for(r2b.at[s], p2_r.at[s, 2])
+        wait_for(r2b.at[s], d2d_r.at[s])
         for h in HALVES:
             n = ring(h, False)[1]
             grad[slab_of(s), :, pl.ds(HALF * h, HALF)] = (b2[s, h, n] + r2b[s, h, 0] + r2b[s, h, 1]) / 32
@@ -267,7 +302,8 @@
         for j in range(MATS):
             w = weight_of(j)
             vec = jnp.where(lane == j, total(w * w), vec)
-        mv_own[slab_of(SLABS - 1), THIRD, LANES:PAIR] = vec
+        mv_own[slab_of(0), THIRD, LANES:PAIR] = vec
+        mv_own[slab_of(0), THIRD, :LANES] = down(dv_mom[...])
 
     def spread(axis, src, dst, ss, rs):
         return [remote(src, dst.at[j], ss, rs, at(axis, j)) for j in OTHERS]
@@ -277,79 +313,77 @@
             cp.start()
 
     def rows_of(k):
-        return pl.ds(0, 3 if isinstance(k, int) and k == slab_of(SLABS - 1) else 2)
-
-    def dv_copies(k):
-        return spread('x', dv_own.at[k], dv_got.at[k], sent.at[3], dv_r.at[k])
+        return pl.ds(0, 3 if k == slab_of(0) else 2)
+
+    def dv_copies(n):
+        return spread('x', dv_own.at[n], dv_got.at[n], sent.at[3], dv_r.at[n])
 
     def y_copies(k):
         src = mv_own.at[k, rows_of(k)]
-        return [remote(src, mv_y.at[k, j + 4 * other, rows_of(k)], sent.at[4 + rows_of(k).size], y_r.at[k],
+        return [remote(src, mv_y.at[k, j + 4 * other, rows_of(k)], sent.at[4 + rows_of(k).size], ld_sem.at[k],
                        at('y', j, other) if j else at('c', 1)) for j in range(4) for other in HALVES if j or other]
 
     def z_copies(k):
-        return [remote(mv_two.at[k, rows_of(k)], mv_z.at[k, j, rows_of(k)], sent.at[6 + rows_of(k).size], z_r.at[k], at('z', j))
+        return [remote(mv_two.at[k, rows_of(k)], mv_z.at[k, j, rows_of(k)], sent.at[6 + rows_of(k).size], whole.at[k], at('z', j))
                 for j in OTHERS]
 
     def sums(k):
         g = grad[k]
         s = g * g + EPS_SQ
         mv_own[k, FIRST] = down(s)
-
-        def wide():
-            dv_own[k] = jnp.where(lane == k, along(s), 0.0)
-
-        def thin():
-            dv = jnp.zeros((BLK, LANES), F32)
-            for q in range(4):
-                dv = jnp.where(lane == 4 * k - 18 + q, along(jnp.where(of_mat(q), s, 0.0)), dv)
-            dv_own[k] = dv
-        choose(k < WIDE, wide, thin)
-        start(dv_copies(k))
+        if k < WIDE:
+            return jnp.where(lane == k, along(s), 0.0)
+        dv = jnp.zeros((BLK, LANES), F32)
+        for q in range(4):
+            low = HALF * (q // 2)
+            t = jnp.where(of_mat(q)[:, low:low + HALF], s[:, low:low + HALF], 0.0)
+            dv = jnp.where(lane == 4 * k - 18 + q, along(t), dv)
+        return dv
 
     def mats_of(k):
-        low = jnp.where(k < WIDE, k, 4 * k - 18)
-        return jnp.logical_and(lane >= low, lane < jnp.where(k < WIDE, k + 1, 4 * k - 14))
-
-    def data_side(k):
-        mine = mats_of(k)
-        wait_for(dv_got.at[k, THREE], dv_r.at[k])
-        got = (dv_own[k] + dv_got[k, 2]) + (dv_got[k, 1] + dv_got[k, 3])
+        low, high = (k, k + 1) if k < WIDE else (4 * k - 18, 4 * k - 14)
+        return jnp.logical_and(lane >= low, lane < high)
+
+    def finish(n):
+        dv = jnp.zeros((BLK, LANES), F32)
+        for s in GROUPS[n]:
+            stage_sum(s)
+            dv = dv + sums(slab_of(s))
+        dv_own[n] = dv
+        start(dv_copies(n))
+
+    def data(n):
+        wait_for(dv_got.at[n, THREE], dv_r.at[n])
+        got = (dv_own[n] + dv_got[n, 2]) + (dv_got[n, 1] + dv_got[n, 3])
         new = BETA_TWO * dv_mom[...] + (1.0 - BETA_TWO) * (got / count)
+        mine = lane < 0
+        for s in GROUPS[n]:
+            mine = jnp.logical_or(mine, mats_of(slab_of(s)))
         dv_all[...] = jnp.where(mine, new, dv_all[...])
-        if rows_of(k).size == 3:
-            mv_own[k, THIRD, :LANES] = down(dv_all[...])
         inv = 1.0 / jnp.sqrt(jnp.where(mine, new, 1.0))
-
-        def column(j):
-            return along(jnp.where(lane == j, inv, 0.0))
-
-        def scaled(factor):
-            q = grad[k] * factor
-            grad[k] = q
-            q = q * UP
-            mv_own[k, SECOND] = down(q * q)
-
-        def wide():
-            scaled(column(k))
-
-        def thin():
-            factor = column(4 * k - 15)
-            for q in (2, 1, 0):
-                factor = jnp.where(col < THIN * q + THIN, column(4 * k - 18 + q), factor)
-            scaled(factor)
-        choose(k < WIDE, wide, thin)
-        start(y_copies(k))
+        for s in GROUPS[n]:
+            k = slab_of(s)
+            if k < WIDE:
+                factor = inv[:, k:k + 1]
+            else:
+                factor = inv[:, 4 * k - 15:4 * k - 14]
+                for q in reversed(range(3)):
+                    factor = jnp.where(col < THIN * q + THIN, inv[:, 4 * k - 18 + q:4 * k - 17 + q], factor)
+            g = grad[k] * factor
+            grad[k] = g
+            g = g * UP
+            mv_own[k, SECOND] = down(g * g)
+            start(y_copies(k))
 
     def stage_z(k):
-        wait_for(mv_y.at[k, pl.ds(1, 7), rows_of(k)], y_r.at[k])
+        wait_for(mv_y.at[k, SEVEN, rows_of(k)], ld_sem.at[k])
         one = [mv_own[k] + mv_y[k, 4]] + [mv_y[k, j] + mv_y[k, 4 + j] for j in OTHERS]
         mv_two[k] = (one[0] + one[2]) + (one[1] + one[3])
         start(z_copies(k))
 
     def model_side(k):
         mine = mats_of(k)
-        wait_for(mv_z.at[k, THREE, rows_of(k)], z_r.at[k])
+        wait_for(mv_z.at[k, THREE, rows_of(k)], whole.at[k])
         v = (mv_two[k] + mv_z[k, 2]) + (mv_z[k, 1] + mv_z[k, 3])
         new = BETA_TWO * mv_mom[k] + (1.0 - BETA_TWO) * (v[FIRST] / D)
         mv_new[k] = new
@@ -358,9 +392,11 @@
         a = a * a
         u = grad[k] * inv
 
+        by_data = (1.0 - BETA_TWO) * (v[FIRST] / (FF if k < WIDE else D))
+
         def wide():
             sc_own[FIRST] = jnp.where(mine, total(a), sc_own[FIRST])
-            sc_own[SECOND] = jnp.where(mine, total(new), sc_own[SECOND])
+            sc_own[SECOND] = jnp.where(mine, total(by_data if k < 4 else new), sc_own[SECOND])
             grad[k] = u
 
         def thin():
@@ -368,7 +404,7 @@
             for q in range(4):
                 j = 4 * k - 18 + q
                 upd = jnp.where(lane == j, total(jnp.where(of_mat(q), a, 0.0)), upd)
-                row = jnp.where(lane == j, total(jnp.where(of_mat(q), new, 0.0)), row)
+                row = jnp.where(lane == j, total(jnp.where(of_mat(q), by_data if j < 15 else new, 0.0)), row)
                 if q % 2 == 0:
                     gsm[j - WIDE] = u[:, THIN * q:THIN * q + THIN]
                 else:
@@ -377,14 +413,8 @@
             sc_own[SECOND] = row
         choose(k < WIDE, wide, thin)
         if rows_of(k).size == 3:
-            by_model = jnp.logical_or(jnp.logical_and(lane >= 4, lane < 6), lane >= 15)
-            sc_own[SECOND] = jnp.where(by_model, sc_own[SECOND], v[THIRD, :LANES] / 4)
             sc_own[THIRD] = v[THIRD, LANES:PAIR]
-
-    def by_parity(fn):
-        def stage(s):
-            choose(lax.rem(s, 2) == 0, lambda: fn(s, 0), lambda: fn(s, 1))
-        return stage
+            sc_own[FOURTH] = v[THIRD, :LANES]
 
     def turn(s):
         stage_turn(s, s % 2)
@@ -392,82 +422,54 @@
     def relay2(s):
         relay(False, s, s % 2)
 
-    def finish(s):
-        stage_sum(s)
-        sums(slab_of(s))
-
     def relay1(s):
         relay(True, s, 0)
 
-    def data(s):
-        data_side(slab_of(s))
-
     def to_z(s):
         stage_z(slab_of(s))
 
     def model(s):
         model_side(slab_of(s))
 
-    early = ((0, stage_split), (LAG_ADD, stage_add), (LAG_RELAY, relay1))
-    late = ((LAG_TURN, by_parity(stage_turn)), (LAG_RELAY2, by_parity(lambda s, flip: relay(False, s, flip))),
-            (LAG_SUM, finish), (LAG_DATA, data), (LAG_Z, to_z), (LAG_MODEL, model))
+    first_split()
+    for cp in [loads[slab_of(j)] for j in range(2, SLABS)] + loads[SLABS:] + small:
+        cp.start()
+    first_add()
 
     def trip(i, carry):
-        for lag, stage in early:
-            @pl.when(i >= lag)
-            def _(lag=lag, stage=stage):
-                stage(i - lag)
+        @pl.when(i > 1)
+        def _():
+            stage_add(i - 1)
+        stage_split(i)
+
+        @pl.when(i > 1)
+        def _():
+            relay1(i - 2)
 
         @pl.when(i == 1)
         def _():
             make_pick()
-        for lag, stage in late:
-            @pl.when(jnp.logical_and(i >= lag, i < HELD + lag))
-            def _(lag=lag, stage=stage):
-                stage(i - lag)
-
-        @pl.when(i == LAG_TURN)
+
+        @pl.when(i == 3)
         def _():
             prepare()
         return carry
-    lax.fori_loop(0, STEPS, trip, 0)
-
-    last = STEPS - 1
-    mids = range(HELD, last - 1)
-    held = range(HELD, last)
-
-    def rest(i):
-        for lag, stage in ((LAG_TURN, turn), (LAG_RELAY2, relay2), (LAG_SUM, finish), (LAG_DATA, data), (LAG_Z, to_z),
-                           (LAG_MODEL, model)):
-            if 0 <= i - lag < HELD:
-                stage(i - lag)
+    lax.fori_loop(1, STEPS, trip, 0)
 
     def each(stage, steps):
         for s in steps:
             stage(s)
+
+    last = STEPS - 1
     stage_add(last)
     relay1(last - 1)
     relay1(last)
-    each(turn, mids)
-    rest(STEPS)
-    turn(last - 1)
-    turn(last)
-    each(relay2, mids)
-    rest(STEPS + 1)
-    relay2(last - 1)
-    relay2(last)
-    rest(STEPS + 2)
-    each(finish, mids)
-    finish(last - 1)
-    rest(STEPS + 3)
-    finish(last)
-    rest(STEPS + 4)
-    each(data, held)
-    data(last)
-    each(to_z, held)
-    to_z(last)
-    each(model, held)
-    model(last)
+    for stage in (turn, relay2):
+        each(stage, range(STEPS))
+    for stage in (finish, data):
+        each(stage, range(len(GROUPS)))
+    for stage in (to_z, model):
+        each(stage, range(STEPS))
 
     sc_cp = spread('x', sc_own, sc_got, sent.at[SLABS + 1], sc_r.at[0])
     start(sc_cp)
@@ -494,18 +496,19 @@
     r_o_n[...] = thin_a[9:12, :THIN]
 
     few = STEPS - 1
-    for j, ref in enumerate((s0, s0.at[:, :, pl.ds(0, 3)], b2.at[:, :, pl.ds(0, 3)], dv_got.at[:, pl.ds(0, 3)])):
+    for j, ref in enumerate((s0, s0.at[:, :, TRIO], b2.at[:, :, TRIO], dv_got.at[:, TRIO])):
         wait_for(ref, sent.at[j])
-    wait_for(mv_y.at[pl.ds(0, few), pl.ds(1, 7), pl.ds(0, 2)], sent.at[6])
-    wait_for(mv_y.at[0, pl.ds(1, 7), pl.ds(0, 3)], sent.at[7])
-    wait_for(mv_z.at[pl.ds(0, few), THREE, pl.ds(0, 2)], sent.at[8])
-    wait_for(mv_z.at[0, THREE, pl.ds(0, 3)], sent.at[9])
+    wait_for(mv_y.at[pl.ds(0, few), SEVEN, DUO], sent.at[6])
+    wait_for(mv_y.at[0, SEVEN, TRIO], sent.at[7])
+    wait_for(mv_z.at[pl.ds(0, few), THREE, DUO], sent.at[8])
+    wait_for(mv_z.at[0, THREE, TRIO], sent.at[9])
 
     wait_for(sc_got.at[THREE], sc_r.at[0])
     sc = (sc_own[...] + sc_got[2]) + (sc_got[1] + sc_got[3])
     full = jnp.where(lane < WIDE, FF * D, D * D)
     rows = jnp.where(jnp.logical_and(lane >= 4, lane < 6), FF, D)
-    row_mean = sc[SECOND] / rows
+    by_model = jnp.logical_or(jnp.logical_and(lane >= 4, lane < 6), lane >= 15)
+    row_mean = (sc[SECOND] + jnp.where(by_model, 0.0, BETA_TWO * (sc[FOURTH] / 4))) / rows
     upd_rms = jnp.sqrt(row_mean * (sc[FIRST] / full))
     w_rms = jnp.sqrt(sc[THIRD] / full)
     scale = LR_BASE * jnp.maximum(1e-3, w_rms) * (jnp.sqrt(row_mean) / jnp.maximum(1.0, upd_rms))
@@ -555,10 +558,10 @@
                 vm(THIN, HALF), pltpu.VMEM((2, THIN, HALF), jnp.bfloat16)]
             + [vm(*a.shape) for n, a in enumerate(small) if n % 3 == 0] + [vm(*a.shape) for n, a in enumerate(small) if n % 3]
             + [vm(LANES, LANES), vm(16, PAIR), vm(16, PAIR), vm(BLK, LANES), vm(BLK, LANES),
-               vm(SLABS, BLK, LANES), vm(SLABS, 4, BLK, LANES), vm(SLABS, 1, DIM), vm(SLABS, 1, DIM),
+               vm(len(GROUPS), BLK, LANES), vm(len(GROUPS), 4, BLK, LANES), vm(SLABS, 1, DIM), vm(SLABS, 1, DIM),
                vm(SLABS, 4, DIM), vm(SLABS, 8, 4, DIM), vm(SLABS, 4, DIM), vm(SLABS, 4, 4, DIM), vm(8, LANES), vm(4, 8, LANES),
-               DMA((SLABS + 1,)), DMA((len(small),)), DMA((SLABS + 2,)), DMA((STEPS, 2)), DMA((STEPS, 3)), DMA((STEPS, 3)),
-               DMA((SLABS,)), DMA((SLABS,)), DMA((SLABS,)), DMA((1,))],
+               DMA((SLABS + 1 + 2 * PARTS,)), DMA((len(small),)), DMA((SLABS + 2,)), DMA((2, PARTS)), DMA((STEPS,)), DMA((STEPS,)), DMA((STEPS,)),
+               DMA((len(GROUPS),)), DMA((1,))],
             compiler_params=pltpu.CompilerParams(
                 collective_id=0, has_side_effects=True, vmem_limit_bytes=58_000_000),
             name='adafactor',

time: 84.2 us -> 82.5 us (0.980)
  Pallas kernels: 83.4 us -> 81.7 us
    pallas_call x1, Pallas kernels: 82.4 us -> 80.7 us  [step_all(): pl.pallas_call(kernel, out_shape=held, in_specs=[pl.BlockSpec(memory_spac...]
where the time goes in v4:
time: 82.5 us; the launch traced here: 82.3 us
  Pallas kernels  81.7 us (99%)
    pallas_call x1, Pallas kernels, step_all(): pl.pallas_call(kernel, out_shape=held, in_specs=[pl.BlockSpec(memory_spac...  80.7 us

profile of v4, /device:TPU:0, one launch (start us, length us, event | category | flops | bytes accessed | tf_op | source)
XLA Modules:
  0.0 82.3 jit_solution(9473334115328632676)
XLA Ops:
  0.7 80.7 %adafactor.1 = (f32[4,24,768]{2,1,0:T(8,128)S(1)}, f32[4,24]{1,0:T(4,128)S(1)}, f32[4,768]{1,0:T(4,128)S(1)}, f32[2,24,768]{2,1,0:T(8,128)S(1)}, f32[2,768]{1,0:...) custom-call(bf16[4,768,768]{2,1,0:T(8,128)(2,1)} %bitcast.12, ...), custom_call_target="tpu_custom_call" | custom-call | tf_op jit(solution)/shard_map/adafactor/pallas_call | solution.py:547
  81.3 1.0 %write_out.1 = (f32[4,24,768]{2,1,0:T(8,128)}, f32[4,24]{1,0:T(4,128)}, f32[4,768]{1,0:T(4,128)}, f32[2,24,768]{2,1,0:T(8,128)}, f32[2,768]{1,0:T(2,128)}, /*ind...) custom-call(f32[4,24,768]{2,1,0:T(8,128)S(1)} %get-tuple-element.36., ...), custom_call_target="tpu_custom_call" | custom-call | tf_op jit(solution)/shard_map/write_out/pallas_call | solution.py:569

commit v5 on v4

--- a/solution.py
+++ b/solution.py
@@ -34,7 +34,7 @@
 OTHERS = (1, 2, 3)
 HALVES = range(2)
 THREE, SEVEN = pl.ds(1, 3), pl.ds(1, 7)
-DUO, TRIO = pl.ds(0, 2), pl.ds(0, 3)
+DUO, TRIO, FOUR = pl.ds(0, 2), pl.ds(0, 3), pl.ds(0, 4)
 FIRST, SECOND, THIRD, FOURTH = (slice(n, n + 1) for n in range(4))
 IN, OUT, QKV, O = slice(4), slice(4, 6), slice(6, 15), slice(15, 18)
 
@@ -70,7 +70,7 @@
            xin, s0, r0, r1a, r1b, b2, r2a, r2b, grad, gsm, pick_f, pick, vw_in, vw_out, vw_qkv, vw_o,
            vr_in, vc_in, vr_out, vc_out, vr_qkv, vc_qkv, vr_o, vc_o,
            square, thin_a, thin_b, dv_mom, dv_all, dv_own, dv_got, mv_mom, mv_new, mv_own, mv_y, mv_two, mv_z,
-           sc_own, sc_got, ld_sem, sm_sem, sent, first_r, d2d_r, passed, whole, dv_r, sc_r):
+           sc_own, sc_got, ld_sem, sm_sem, sent, first_r, d2d_r, passed, whole, dv_r, sc_r, far):
     d = lax.axis_index('data')
     x = lax.axis_index('model')
     core = lax.rem(d, 2)
@@ -96,14 +96,14 @@
               local(g_o, xin.at[SLABS - 1, pl.ds(THIN, DIM - THIN)], ld_sem.at[SLABS])]
     small = [(w_in, vw_in), (w_out, vw_out), (w_qkv, vw_qkv), (w_o, vw_o), (r_in, vr_in), (c_in, vc_in),
              (r_out, vr_out), (c_out, vc_out), (r_qkv, vr_qkv), (c_qkv, vc_qkv), (r_o, vr_o), (c_o, vc_o)]
-    small = [local(s, t, sm_sem.at[j]) for j, (s, t) in enumerate(small)]
+    small = [local(s, t, sm_sem.at[j] if j < 6 else sent.at[j - 1]) for j, (s, t) in enumerate(small)]
     loads[0] = [local(g_in.at[0, :, span(h, c)], xin.at[0, :, span(h, c)], ld_sem.at[SLABS + 1 + h + 2 * c])
                 for c in range(PARTS) for h in HALVES]
     for cp in loads[0] + [loads[1]]:
         cp.start()
 
     barrier = pltpu.get_barrier_semaphore()
-    peers = [at('c', 1)] + [at(a, j) for a in 'yzx' for j in OTHERS] + [at('y', j, 1) for j in OTHERS]
+    peers = [at('c', 1)] + [at(a, j) for a in 'yzx' for j in OTHERS if j % 2]
     for p in peers:
         pl.semaphore_signal(barrier, inc=1, device_id=p, device_id_type=MESH)
 
@@ -274,6 +274,7 @@
     def prepare():
         for cp in small:
             cp.wait()
+        pl.semaphore_wait(far, 2)
         square[...] = jnp.zeros_like(square)
         square[IN, :BLK] = vr_in[...]
         square[OUT, :BLK] = vc_out[...]
@@ -330,7 +331,6 @@
     def sums(k):
         g = grad[k]
         s = g * g + EPS_SQ
-        mv_own[k, FIRST] = down(s)
         if k < WIDE:
             return jnp.where(lane == k, along(s), 0.0)
         dv = jnp.zeros((BLK, LANES), F32)
@@ -351,6 +351,10 @@
             dv = dv + sums(slab_of(s))
         dv_own[n] = dv
         start(dv_copies(n))
+        for s in GROUPS[n]:
+            k = slab_of(s)
+            g = grad[k]
+            mv_own[k, FIRST] = down(g * g + EPS_SQ)
 
     def data(n):
         wait_for(dv_got.at[n, THREE], dv_r.at[n])
@@ -432,6 +436,9 @@
         model_side(slab_of(s))
 
     first_split()
+    for j in OTHERS:
+        if j % 2:
+            pl.semaphore_signal(far, inc=1, device_id=at('x', j), device_id_type=MESH)
     for cp in [loads[slab_of(j)] for j in range(2, SLABS)] + loads[SLABS:] + small:
         cp.start()
     first_add()
@@ -471,7 +478,7 @@
     for stage in (to_z, model):
         each(stage, range(STEPS))
 
-    sc_cp = spread('x', sc_own, sc_got, sent.at[SLABS + 1], sc_r.at[0])
+    sc_cp = [remote(sc_own.at[FOUR], sc_got.at[j, FOUR], sent.at[SLABS + 1], sc_r.at[0], at('x', j)) for j in OTHERS]
     start(sc_cp)
 
     square[:BLK] = dv_all[...]
@@ -503,7 +510,7 @@
     wait_for(mv_z.at[pl.ds(0, few), THREE, DUO], sent.at[8])
     wait_for(mv_z.at[0, THREE, TRIO], sent.at[9])
 
-    wait_for(sc_got.at[THREE], sc_r.at[0])
+    wait_for(sc_got.at[THREE, FOUR], sc_r.at[0])
     sc = (sc_own[...] + sc_got[2]) + (sc_got[1] + sc_got[3])
     full = jnp.where(lane < WIDE, FF * D, D * D)
     rows = jnp.where(jnp.logical_and(lane >= 4, lane < 6), FF, D)
@@ -517,7 +524,7 @@
         new = weight_of(j) - scale[:, j:j + 1] * upd
         n, i = place(j)
         (w_in_n, w_out_n, w_qkv_n, w_o_n)[n][i] = new
-    wait_for(sc_got.at[THREE], sent.at[SLABS + 1])
+    wait_for(sc_got.at[THREE, FOUR], sent.at[SLABS + 1])
 
 
 def write_out(*refs):
@@ -560,8 +567,8 @@
             + [vm(LANES, LANES), vm(16, PAIR), vm(16, PAIR), vm(BLK, LANES), vm(BLK, LANES),
                vm(len(GROUPS), BLK, LANES), vm(len(GROUPS), 4, BLK, LANES), vm(SLABS, 1, DIM), vm(SLABS, 1, DIM),
                vm(SLABS, 4, DIM), vm(SLABS, 8, 4, DIM), vm(SLABS, 4, DIM), vm(SLABS, 4, 4, DIM), vm(8, LANES), vm(4, 8, LANES),
-               DMA((SLABS + 1 + 2 * PARTS,)), DMA((len(small),)), DMA((SLABS + 2,)), DMA((2, PARTS)), DMA((STEPS,)), DMA((STEPS,)), DMA((STEPS,)),
-               DMA((len(GROUPS),)), DMA((1,))],
+               DMA((SLABS + 1 + 2 * PARTS,)), DMA((6,)), DMA((SLABS + 2,)), DMA((2, PARTS)), DMA((STEPS,)), DMA((STEPS,)), DMA((STEPS,)),
+               DMA((len(GROUPS),)), DMA((1,)), pltpu.SemaphoreType.REGULAR],
             compiler_params=pltpu.CompilerParams(
                 collective_id=0, has_side_effects=True, vmem_limit_bytes=58_000_000),
             name='adafactor',

time: 82.5 us -> 81.9 us (level)
  no operation moved by 1% of the time
where the time goes in v5:
time: 81.9 us; the launch traced here: 81.8 us
  Pallas kernels  81.2 us (99%)
    pallas_call x1, Pallas kernels, step_all(): pl.pallas_call(kernel, out_shape=held, in_specs=[pl.BlockSpec(memory_spac...  80.2 us

profile of v5, /device:TPU:0, one launch (start us, length us, event | category | flops | bytes accessed | tf_op | source)
XLA Modules:
  0.0 81.8 jit_solution(15727523195904392408)
XLA Ops:
  0.7 80.2 %adafactor.1 = (f32[4,24,768]{2,1,0:T(8,128)S(1)}, f32[4,24]{1,0:T(4,128)S(1)}, f32[4,768]{1,0:T(4,128)S(1)}, f32[2,24,768]{2,1,0:T(8,128)S(1)}, f32[2,768]{1,0:...) custom-call(bf16[4,768,768]{2,1,0:T(8,128)(2,1)} %bitcast.12, ...), custom_call_target="tpu_custom_call" | custom-call | tf_op jit(solution)/shard_map/adafactor/pallas_call | solution.py:554
  80.8 1.0 %write_out.1 = (f32[4,24,768]{2,1,0:T(8,128)}, f32[4,24]{1,0:T(4,128)}, f32[4,768]{1,0:T(4,128)}, f32[2,24,768]{2,1,0:T(8,128)}, f32[2,768]{1,0:T(2,128)}, /*ind...) custom-call(f32[4,24,768]{2,1,0:T(8,128)S(1)} %get-tuple-element.36., ...), custom_call_target="tpu_custom_call" | custom-call | tf_op jit(solution)/shard_map/write_out/pallas_call | solution.py:576

commit v6 on v5

--- a/solution.py
+++ b/solution.py
@@ -31,7 +31,7 @@
 PARTS = 3
 
 
-OTHERS = (1, 2, 3)
+OTHERS = (2, 1, 3)
 HALVES = range(2)
 THREE, SEVEN = pl.ds(1, 3), pl.ds(1, 7)
 DUO, TRIO, FOUR = pl.ds(0, 2), pl.ds(0, 3), pl.ds(0, 4)
@@ -322,7 +322,7 @@
     def y_copies(k):
         src = mv_own.at[k, rows_of(k)]
         return [remote(src, mv_y.at[k, j + 4 * other, rows_of(k)], sent.at[4 + rows_of(k).size], ld_sem.at[k],
-                       at('y', j, other) if j else at('c', 1)) for j in range(4) for other in HALVES if j or other]
+                       at('y', j, other) if j else at('c', 1)) for j in OTHERS + (0,) for other in HALVES if j or other]
 
     def z_copies(k):
         return [remote(mv_two.at[k, rows_of(k)], mv_z.at[k, j, rows_of(k)], sent.at[6 + rows_of(k).size], whole.at[k], at('z', j))
@@ -381,7 +381,7 @@
 
     def stage_z(k):
         wait_for(mv_y.at[k, SEVEN, rows_of(k)], ld_sem.at[k])
-        one = [mv_own[k] + mv_y[k, 4]] + [mv_y[k, j] + mv_y[k, 4 + j] for j in OTHERS]
+        one = [mv_own[k] + mv_y[k, 4]] + [mv_y[k, j] + mv_y[k, 4 + j] for j in sorted(OTHERS)]
         mv_two[k] = (one[0] + one[2]) + (one[1] + one[3])
         start(z_copies(k))
 

time: 81.9 us -> 81.7 us (level)
  no operation moved by 1% of the time
where the time goes in v6:
time: 81.7 us; the launch traced here: 81.6 us
  Pallas kernels  80.9 us (99%)
    pallas_call x1, Pallas kernels, step_all(): pl.pallas_call(kernel, out_shape=held, in_specs=[pl.BlockSpec(memory_spac...  79.9 us

profile of v6, /device:TPU:0, one launch (start us, length us, event | category | flops | bytes accessed | tf_op | source)
XLA Modules:
  0.0 81.6 jit_solution(12089125200236974093)
XLA Ops:
  0.7 79.9 %adafactor.1 = (f32[4,24,768]{2,1,0:T(8,128)S(1)}, f32[4,24]{1,0:T(4,128)S(1)}, f32[4,768]{1,0:T(4,128)S(1)}, f32[2,24,768]{2,1,0:T(8,128)S(1)}, f32[2,768]{1,0:...) custom-call(bf16[4,768,768]{2,1,0:T(8,128)(2,1)} %bitcast.12, ...), custom_call_target="tpu_custom_call" | custom-call | tf_op jit(solution)/shard_map/adafactor/pallas_call | solution.py:554
  80.6 1.0 %write_out.1 = (f32[4,24,768]{2,1,0:T(8,128)}, f32[4,24]{1,0:T(4,128)}, f32[4,768]{1,0:T(4,128)}, f32[2,24,768]{2,1,0:T(8,128)}, f32[2,768]{1,0:T(2,128)}, /*ind...) custom-call(f32[4,24,768]{2,1,0:T(8,128)S(1)} %get-tuple-element.36., ...), custom_call_target="tpu_custom_call" | custom-call | tf_op jit(solution)/shard_map/write_out/pallas_call | solution.py:576
